TPU v7x, 32 devices: a whole 2x2x4 slice. The times are simulated.
32 devices in a mesh: grp: 4 (over x, core), dev: 8 (over z, y).
Axes of the slice: x: 2, y: 2, z: 4, core: 2. Of those that a mesh axis runs over, the one named last changes fastest.
Arguments:
- energies: bfloat16 [4096, 32768], P(('grp', 'dev')), may hold values from -48 to 48
- triples: int32 [4096, 3], P(('grp', 'dev')), may hold values from 0 to 113, as said below
- pair_surfaces: float32 [7200, 1024], P('dev'), may hold values from -24 to 24
- pair_slot: int32 [114, 114], replicated, may hold values from 0 to 7199, as said below
- single_surfaces: float32 [120, 32], P('dev'), may hold values from -12 to 12
- modals: float32 [120, 512], P('dev'), may hold values from -1 to 1
- mode_slot: int32 [114], replicated, may hold values from 0 to 119, as said below
Outputs:
- coefficients: bfloat16 [4096, 4096], P(('grp', 'dev'))
- triple_energy: float32 [4096], P(('grp', 'dev'))
- mean_field: float32 [120, 256], P('dev')
Inputs may be any that keep to these rules, and one draw needn't show every extreme that they name: The three modes of a row are distinct. Rows come in blocks of 128, one block to each device in the order of the triples' placement; all rows of a block share their first mode m, and m * (number of groups along grp) // 114 is the block's index along grp. Counting one need for each row and each of its three pairs, the rows of one block need exactly 48 surfaces from each owner along dev, the owner of pair_slot row q being q // 900. `pair_slot`: Symmetric; for two distinct modes it names the row of pair_surfaces that holds their surface, distinct pairs naming distinct rows; the diagonal is 0. `mode_slot`: distinct modes name distinct rows.
All inputs are finite; a program needn't handle non-finite values.
Results may differ from a plain program's by a relative error of at most 0.001.
Values sent between devices are 32-bit elements; how exact they have to be, the bound alone decides.
A program may use at most 128 MiB of HBM per device.

v0:
```python
import jax
import jax.numpy as jnp
import numpy as np
from jax import lax
from jax.experimental import pallas as pl
from jax.experimental.pallas import tpu as pltpu
from jax.sharding import PartitionSpec as P

G = 32
KEEP = 16
S = 16
PAIRS = 4

highest = lax.Precision.HIGHEST


def np_tables():
    orders = np.arange(KEEP, dtype=np.float64)
    points = np.arange(G, dtype=np.float64) + 0.5
    cosines = np.cos(np.pi * orders[:, None] * points[None, :] / G)
    weights = np.where(orders == 0, 1.0, 2.0) / G
    return cosines, weights[:, None] * cosines


COS, FIT = np_tables()
ROWSUM = FIT.astype(np.float32).sum(axis=1, dtype=np.float64)


def split(values):
    values = np.asarray(values, np.float32)
    high = values.astype(jnp.bfloat16)
    return high, (values - high.astype(np.float32)).astype(jnp.bfloat16)


PLAIN = np.einsum("dh,el->hlde", FIT, FIT).reshape(G * G, KEEP * KEEP)
SWAPPED = np.einsum("eh,dl->hlde", FIT, FIT).reshape(G * G, KEEP * KEEP)
eye = np.eye(KEEP)
SPREAD_D = np.einsum("xd,e->xde", eye, np.ones(KEEP)).reshape(KEEP, -1)
SPREAD_E = np.einsum("xe,d->xde", eye, np.ones(KEEP)).reshape(KEEP, -1)
FIRST = np.einsum("xd,e->xde", eye, ROWSUM).reshape(KEEP, -1)
SECOND = np.einsum("xe,d->xde", eye, ROWSUM).reshape(KEEP, -1)
GROUND = np.einsum("cg,s->gsc", COS, np.arange(S) == 0).reshape(G * S, KEEP)


def dot(a, b, precision=None):
    return jnp.dot(a, b, precision=precision, preferred_element_type=jnp.float32)


def pair_kernel(surf_ref, high_ref, low_ref, out_ref):
    values = surf_ref[...]
    top = values.astype(jnp.bfloat16)
    rest = (values - top.astype(jnp.float32)).astype(jnp.bfloat16)
    fitted = dot(top, high_ref[...]) + dot(top, low_ref[...]) + dot(rest, high_ref[...])
    out_ref[0] = fitted[:, : KEEP * KEEP]
    out_ref[1] = fitted[:, KEEP * KEEP :]


def pair_table(pair_surfaces):
    rows = pair_surfaces.shape[0]
    block = min(304, rows)
    steps = -(-rows // block)
    padded = steps * block
    high, low = split(np.concatenate([PLAIN, SWAPPED], axis=1))
    whole = lambda a: pl.BlockSpec(a.shape, lambda i: (0, 0))
    table = pl.pallas_call(
        pair_kernel,
        grid=(steps,),
        in_specs=[pl.BlockSpec((block, G * G), lambda i: (i, 0)), whole(high), whole(low)],
        out_specs=pl.BlockSpec((2, block, KEEP * KEEP), lambda i: (0, i, 0)),
        out_shape=jax.ShapeDtypeStruct((2, padded, KEEP * KEEP), jnp.float32),
        cost_estimate=pl.CostEstimate(
            flops=12 * rows * G * G * KEEP * KEEP, bytes_accessed=4 * rows * G * G, transcendentals=0
        ),
    )(pair_surfaces, jnp.asarray(high), jnp.asarray(low))
    return table.reshape(2 * padded, KEEP * KEEP), padded


def fit_kernel(scale_ref, front_ref, back_ref, high_ref, low_ref, acc):
    step = pl.program_id(0)
    number = front_ref.shape[0]
    high, low = high_ref[...], low_ref[...]

    @pl.when(step == 0)
    def _():
        acc[...] = jnp.zeros_like(acc)

    sums, differences = [], []
    for j in range(PAIRS):
        k = PAIRS - 1 - j
        both = jnp.concatenate(
            [front_ref[:, j * G * G : (j + 1) * G * G], back_ref[:, k * G * G : (k + 1) * G * G]],
            axis=0,
        )
        planes = dot(both, high) + dot(both, low)
        sums.append(planes[:number] + planes[number:])
        differences.append(planes[:number] - planes[number:])
    for c in range(KEEP):
        parts = sums if c % 2 == 0 else differences
        total = acc[c]
        for j in range(PAIRS):
            total += scale_ref[c, step * PAIRS + j] * parts[j]
        acc[c] = total


def field_kernel(
    acc, pair_ref, column_ref, row_ref, table_ref,
    spread_d_ref, spread_e_ref, first_ref, second_ref, expand_ref,
    coef_ref, energy_ref, partial_ref,
):
    number = acc.shape[1]
    area = KEEP * KEEP
    slots = table_ref.shape[0]
    hits = (column_ref[...] == lax.broadcasted_iota(jnp.int32, (3 * number, slots), 1))
    taken = dot(hits.astype(jnp.float32), table_ref[...], highest)
    ground, single = taken[:, :KEEP], taken[:, KEEP:]
    g1, g2, g3 = (ground[i * number : (i + 1) * number] for i in range(3))
    s1, s2, s3 = (single[i * number : (i + 1) * number] for i in range(3))
    g2e = dot(g2, spread_d_ref[...], highest)
    g3e = dot(g3, spread_e_ref[...], highest)
    weight = g2e * g3e
    p12 = pair_ref[:number] + dot(s1, first_ref[...], highest) + dot(s2, second_ref[...], highest)
    p13 = pair_ref[number : 2 * number] + dot(s3, second_ref[...], highest)
    p23 = pair_ref[2 * number :]

    def halves(values):
        top = values.astype(jnp.bfloat16).astype(jnp.float32)
        return top, values - top

    pieces = halves(p12) + halves(p13)
    lane = lax.broadcasted_iota(jnp.int32, (number, KEEP), 1)
    f1 = jnp.zeros((number, KEEP), jnp.float32)
    mixed = jnp.zeros((number, area), jnp.float32)
    for c in range(KEEP):
        left = jnp.concatenate([p[:, c * KEEP : (c + 1) * KEEP] for p in pieces], axis=1)
        correction = dot(left.astype(jnp.bfloat16), expand_ref[...])
        fitted = acc[c] - correction - p23 * float(ROWSUM[c])
        coef_ref[:, c * area : (c + 1) * area] = fitted.astype(jnp.bfloat16)
        f1 = f1 + jnp.where(lane == c, jnp.sum(fitted * weight, axis=1, keepdims=True), 0.0)
        mixed = mixed + g1[:, c : c + 1] * fitted
    gather = lambda a, b: lax.dot_general(
        a, b, (((1,), (1,)), ((), ())), precision=highest, preferred_element_type=jnp.float32
    )
    f2 = gather(mixed * g3e, spread_d_ref[...])
    f3 = gather(mixed * g2e, spread_e_ref[...])
    energy_ref[...] = jnp.sum(f1 * g1, axis=1, keepdims=True)
    fields = jnp.concatenate([f1, f2, f3], axis=0)
    hits_t = (row_ref[...] == lax.broadcasted_iota(jnp.int32, (slots, 3 * number), 0))
    partial_ref[...] = dot(hits_t.astype(jnp.float32), fields, highest)


def fit(energies):
    number = energies.shape[0]
    steps = G // 2 // PAIRS
    blocks = G // PAIRS
    high, low = split(PLAIN)
    whole = lambda a: pl.BlockSpec(a.shape, lambda i: (0, 0))
    width = PAIRS * G * G
    area = KEEP * KEEP
    return pl.pallas_call(
        fit_kernel,
        grid=(steps,),
        in_specs=[
            pl.BlockSpec(memory_space=pltpu.SMEM),
            pl.BlockSpec((number, width), lambda i: (0, i)),
            pl.BlockSpec((number, width), lambda i: (0, blocks - 1 - i)),
            whole(high),
            whole(low),
        ],
        out_specs=pl.BlockSpec((KEEP, number, area), lambda i: (0, 0, 0)),
        out_shape=jax.ShapeDtypeStruct((KEEP, number, area), jnp.float32),
        cost_estimate=pl.CostEstimate(
            flops=4 * number * G * G * G * area, bytes_accessed=2 * number * G * G * G, transcendentals=0
        ),
        compiler_params=pltpu.CompilerParams(dimension_semantics=("arbitrary",)),
    )(jnp.asarray(FIT.astype(np.float32)), energies, energies, jnp.asarray(high), jnp.asarray(low))


def fields(fitted, pair_terms, slot_ids, table):
    number = fitted.shape[1]
    first, second = FIRST.astype(np.float32), SECOND.astype(np.float32)
    spread_d, spread_e = SPREAD_D.astype(np.float32), SPREAD_E.astype(np.float32)
    expand = np.concatenate([first, first, second, second], axis=0).astype(jnp.bfloat16)
    return pl.pallas_call(
        field_kernel,
        out_shape=[
            jax.ShapeDtypeStruct((number, KEEP * KEEP * KEEP), jnp.bfloat16),
            jax.ShapeDtypeStruct((number, 1), jnp.float32),
            jax.ShapeDtypeStruct((table.shape[0], KEEP), jnp.float32),
        ],
    )(
        fitted, pair_terms, slot_ids[:, None], slot_ids[None, :], table,
        jnp.asarray(spread_d), jnp.asarray(spread_e), jnp.asarray(first), jnp.asarray(second),
        jnp.asarray(expand),
    )


def body(energies, triples, pair_surfaces, pair_slot, single_surfaces, modals, mode_slot):
    devices = lax.axis_size("dev")
    groups = lax.axis_size("grp")
    number = triples.shape[0]
    pair_rows = pair_surfaces.shape[0]
    mode_rows = modals.shape[0]
    modes = mode_slot.shape[0]
    capacity = 3 * number // devices
    cosines = jnp.asarray(COS.astype(np.float32))
    fitter = jnp.asarray(FIT.astype(np.float32))

    pairs, padded = pair_table(pair_surfaces)

    local_ground = jnp.dot(modals * modals, jnp.asarray(GROUND.astype(np.float32)), precision=highest)
    local_single = jnp.dot(single_surfaces, fitter.T, precision=highest)
    local_modes = jnp.concatenate([local_ground, local_single], axis=1).reshape(1, -1)

    a1, a2, a3 = triples[:, 0], triples[:, 1], triples[:, 2]
    lower = jnp.concatenate([a1, a1, a2])
    upper = jnp.concatenate([a2, a3, a3])
    mode_ids = jnp.arange(modes, dtype=jnp.int32)
    lines = jnp.dot(
        (lower[:, None] == mode_ids[None, :]).astype(jnp.float32),
        pair_slot.astype(jnp.float32),
        precision=highest,
    )
    pair_ids = jnp.sum(jnp.where(upper[:, None] == mode_ids[None, :], lines, 0.0), axis=1)
    pair_ids = (pair_ids + 0.5).astype(jnp.int32)
    all_modes = jnp.concatenate([a1, a2, a3])
    slot_ids = jnp.sum(
        jnp.where(all_modes[:, None] == mode_ids[None, :], mode_slot[None, :], 0), axis=1
    )
    owners = pair_ids // pair_rows
    local_rows = pair_ids - owners * pair_rows + jnp.where(lower < upper, 0, padded)
    index = jnp.arange(3 * number, dtype=jnp.int32)
    earlier = (owners[:, None] == owners[None, :]) & (index[:, None] < index[None, :])
    places = owners * capacity + jnp.sum(earlier.astype(jnp.int32), axis=0)
    requests = jnp.sum(jnp.where(places[:, None] == index[None, :], local_rows[:, None], 0), axis=0)

    sent = jnp.concatenate(
        [
            requests.astype(jnp.float32).reshape(devices, capacity),
            jnp.broadcast_to(local_modes, (devices, local_modes.shape[1])),
        ],
        axis=1,
    )
    received = lax.all_to_all(sent, "dev", split_axis=0, concat_axis=0, tiled=True)
    wanted = received[:, :capacity].astype(jnp.int32).reshape(-1)
    table = received[:, capacity:].reshape(devices * mode_rows, 2 * KEEP)
    answers = pairs[wanted].reshape(devices, capacity, KEEP * KEEP)
    arrived = lax.all_to_all(answers, "dev", split_axis=0, concat_axis=0, tiled=True)
    pair_terms = arrived.reshape(devices * capacity, KEEP * KEEP)[places]

    coefficients, energy, partial = fields(fit(energies), pair_terms, slot_ids, table)

    spread = jnp.broadcast_to(
        partial.reshape(1, devices, mode_rows, KEEP), (groups, devices, mode_rows, KEEP)
    ).reshape(groups * devices, mode_rows, KEEP)
    moments = jnp.sum(
        lax.all_to_all(spread, ("grp", "dev"), split_axis=0, concat_axis=0, tiled=True), axis=0
    )
    weighted = jnp.dot(moments, cosines, precision=highest)
    shaped = modals.reshape(mode_rows, G, S)
    mean_field = jnp.einsum("mga,mg,mgb->mab", shaped, weighted, shaped, precision=highest)
    return coefficients, energy.reshape(number), mean_field.reshape(mode_rows, S * S)


def solution(mesh):
    in_specs = (
        P(("grp", "dev"), None),
        P(("grp", "dev"), None),
        P("dev", None),
        P(),
        P("dev", None),
        P("dev", None),
        P(),
    )
    out_specs = (P(("grp", "dev"), None), P(("grp", "dev")), P("dev", None))
    return jax.shard_map(body, mesh=mesh, in_specs=in_specs, out_specs=out_specs, check_vma=False)
```

profile of v0, /device:TPU:0, one launch (start us, length us, event | category | flops | bytes accessed | tf_op | source)
XLA Modules:
  0.0 69.0 jit_solution(17669000749375282564)
XLA Ops:
  0.6 0.8 %slice_bitcast_fusion.1 = (s32[128]{0:T(128)S(1)}, s32[128]{0:T(128)S(1)}, s32[128]{0:T(128)S(1)}) fusion(s32[128,3]{0,1:T(4,128)} %param.21), kind=kLoop, calls=%fused_computation.48 | loop fusion | bytes 3072 | tf_op jit(solution)/shard_map/squeeze | solution.py:214
  1.5 1.2 %fusion = f32[384]{0:T(512)S(1)} fusion(s32[384]{0:T(512)S(1)} %get-tuple-element.18, s32[384]{0:T(512)S(1)} %get-tuple-element.17, s32[114,114]{1,0:T(8,128)} %param.23), kind=kOutput, calls=%fused_computation.4 | convolution fusion | flops 60073284 | bytes 56592 | tf_op jit(solution)/shard_map/dot_general | solution.py:218
  3.1 0.8 %convolution_bitcast_fusion.1 = f32[15,16]{1,0:T(8,128)S(1)} fusion(f32[16,32]{1,0:T(8,128)} %constant.51.clone.scale_ref, f32[15,32]{1,0:T(8,128)S(1)} %copy-done), kind=kOutput, calls=%fused_computation.5 | convolution fusion | flops 92160 | bytes 4928 | tf_op jit(solution)/shard_map/dot_general | solution.py:211
  4.0 1.2 %fusion.6 = f32[15,16]{1,0:T(8,128)S(1)} fusion(f32[512,16]{1,0:T(8,128)} %constant.54.clone, f32[15,512]{1,0:T(8,128)} %param.25), kind=kOutput, calls=%fused_computation.20 | convolution fusion | flops 1482240 | bytes 64448 | tf_op jit(solution)/shard_map/dot_general | solution.py:210
  5.4 0.6 all_to_all.14
  6.1 7.3 %all-to-all-start = ((f32[8,1,528]{2,1,0:T(1,128)}), f32[8,1,528]{2,1,0:T(1,128)S(1)}, u32[]{:S(2)}, u32[]{:S(2)}) async-start(f32[8,1,528]{2,1,0:T(1,128)} %all_to_all.14), calls=%async_computation | async-start | bytes 40960 | tf_op jit(solution)/shard_map/all_to_all | solution.py:243
  13.4 6.5 %shard_map.212 = f32[2,912,256]{2,1,0:T(8,128)} custom-call(f32[900,1024]{1,0:T(8,128)} %surf_ref.1, bf16[1024,512]{1,0:T(8,128)(2,1)} %constant.52.clone.high_ref, bf16[1024,512]{1,0:T(8,128)(2,1)} %constant.53.clone.low_ref), custom_call_target="tpu_custom_call" | custom-call | flops 2831155200 | bytes 3686400 | tf_op jit(solution)/shard_map/pallas_call | solution.py:65
  20.1 3.7 %gather_fusion = f32[384,256]{1,0:T(8,128)} fusion(f32[1824,256]{1,0:T(8,128)} %bitcast.25, s32[1024]{0:T(1024)S(1)} %pad_clamp_fusion.1), kind=kCustom, calls=%fused_computation | custom fusion | bytes 787968 | tf_op jit(solution)/shard_map/gather | solution.py:246
  23.8 5.9 %all-to-all-start.1 = ((f32[8,48,256]{2,1,0:T(8,128)}), f32[8,48,256]{2,1,0:T(8,128)S(1)}, u32[]{:S(2)}, u32[]{:S(2)}) async-start(f32[8,48,256]{2,1,0:T(8,128)} %bitcast.5), calls=%async_computation.1 | async-start | bytes 786432 | tf_op jit(solution)/shard_map/all_to_all | solution.py:247
  29.8 0.8 %broadcast_in_dim.82.column_ref = s32[384,1]{1,0:T(8,128)} reshape(s32[384]{0:T(512)S(1)} %select_reduce_fusion.1) | data formatting | bytes 3072 | tf_op jit(solution)/shard_map/broadcast_in_dim | solution.py:191
  30.6 0.6 broadcast_in_dim.79.row_ref
  31.2 11.5 %shard_map.211.acc = f32[16,128,256]{2,1,0:T(8,128)} custom-call(f32[16,32]{1,0:T(8,128)} %constant.51.clone.scale_ref, bf16[128,32768]{1,0:T(8,128)(2,1)} %back_ref.1, bf16[128,32768]{1,0:T(8,128)(2,1)} %back_ref.1, bf16[1024,256]{1,0:T(8,128)(2,1)} %constant.55.clone.high_ref, bf16[1024,256]{1,0:T(8,128)(2,1)} %constant.56.clone.low_ref), custom_call_target="tpu_custom_call" | custom-call | flops 4294967296 | bytes 8388608 | tf_op jit(solution)/shard_map/pallas_call | solution.py:159
  42.8 0.7 %reshape.210.table_ref = f32[120,32]{1,0:T(8,128)} reshape(f32[8,480]{1,0:T(8,128)S(1)} %slice.25) | data formatting | bytes 30720 | tf_op jit(solution)/shard_map/reshape | solution.py:245
  43.5 2.2 %gather_fusion.1 = f32[384,256]{1,0:T(8,128)} fusion(f32[384,256]{1,0:T(8,128)S(1)} %bitcast.24, s32[1024]{0:T(1024)S(1)} %pad_clamp_fusion), kind=kCustom, calls=%fused_computation.1 | custom fusion | bytes 787968 | tf_op jit(solution)/shard_map/gather | solution.py:248
  45.7 5.3 %shard_map.213 = (bf16[128,4096]{1,0:T(8,128)(2,1)}, f32[128,1]{1,0:T(8,128)}, f32[120,16]{1,0:T(8,128)}) custom-call(f32[16,128,256]{2,1,0:T(8,128)} %shard_map.211.acc, f32[384,256]{1,0:T(8,128)} %gather_fusion.1, s32[384,1]{1,0:T(8,128)} %broadcast_in_dim.82.column_ref, s32[1,384]{1,0:T(1,128)} %broadcast_in_dim.79.row_ref, ...), custom_call_target="tpu_custom_call" | custom-call | tf_op jit(solution)/shard_map/pallas_call | solution.py:183
  51.0 0.8 %reshape.232 = f32[8,15,16]{2,1,0:T(8,128)S(1)} reshape(f32[120,16]{1,0:T(8,128)} %get-tuple-element.8) | data formatting | bytes 15360 | tf_op jit(solution)/shard_map/broadcast_in_dim | solution.py:252
  52.0 0.8 %reshape.244 = f32[32,1,240]{2,1,0:T(1,128)} reshape(f32[32,15,16]{2,1,0:T(8,128)S(1)} %copy.53) | data formatting | bytes 61440
  52.8 6.0 %all-to-all-start.2 = ((f32[32,1,240]{2,1,0:T(1,128)}), f32[32,1,240]{2,1,0:T(1,128)S(1)}, u32[]{:S(2)}, u32[]{:S(2)}) async-start(f32[32,1,240]{2,1,0:T(1,128)} %reshape.244), calls=%async_computation.2 | async-start | bytes 65536 | tf_op jit(solution)/shard_map/all_to_all | solution.py:256
  58.9 1.5 %reduce.2 = f32[128]{0:T(128)} reduce(f32[128,1]{1,0:T(8,128)} %get-tuple-element.7, f32[]{:T(128)} %constant.67), dimensions={1}, to_apply=%get-tuple-element.7.reduce_sub_computation | reduce | bytes 1028 | tf_op jit(solution)/shard_map/pallas_call | solution.py:183
  60.4 5.6 %all-to-all-done.2 = f32[32,1,240]{2,1,0:T(1,128)S(1)} async-done(((f32[32,1,240]{2,1,0:T(1,128)}), f32[32,1,240]{2,1,0:T(1,128)S(1)}, u32[]{:S(2)}, u32[]{:S(2)}) %all-to-all-start.2) | async-done | bytes 30752 | tf_op jit(solution)/shard_map/all_to_all | solution.py:256
  66.0 0.5 broadcast.199
  66.5 0.7 %reduce.5 = f32[32,240]{1,0:T(8,128)S(1)} reduce(f32[32,1,240]{2,1,0:T(1,128)S(1)} %all-to-all-done.2, f32[]{:T(128)} %broadcast.199), dimensions={1}, to_apply=%all_to_all.18.reduce_sub_computation | reduce | bytes 61444 | tf_op jit(solution)/shard_map/all_to_all | solution.py:256
  67.5 0.7 convolution_bitcast_fusion
  68.3 0.7 %reshape.214 = f32[15,256]{1,0:T(8,128)} reshape(f32[15,16,16]{2,1,0:T(8,128)S(1)} %copy.57) | data formatting | bytes 30720 | tf_op jit(solution)/shard_map/reshape | solution.py:261
  (38 shorter events, 1.8 us)
Async XLA Ops:
  0.6 2.5 %copy-start = (f32[15,32]{1,0:T(8,128)S(1)}, f32[15,32]{1,0:T(8,128)}, u32[]{:S(2)}) copy-start(f32[15,32]{1,0:T(8,128)} %param.24) | copy-start | bytes 5764
  6.1 13.9 %all-to-all-start = ((f32[8,1,528]{2,1,0:T(1,128)}), f32[8,1,528]{2,1,0:T(1,128)S(1)}, u32[]{:S(2)}, u32[]{:S(2)}) async-start(f32[8,1,528]{2,1,0:T(1,128)} %all_to_all.14), calls=%async_computation | async-start | bytes 40960 | tf_op jit(solution)/shard_map/all_to_all | solution.py:243
  20.1 9.6 %copy-start.3 = (s32[114]{0:T(128)S(1)}, s32[114]{0:T(128)}, u32[]{:S(2)}) copy-start(s32[114]{0:T(128)} %param.26) | copy-start | bytes 1372
  23.8 19.7 %all-to-all-start.1 = ((f32[8,48,256]{2,1,0:T(8,128)}), f32[8,48,256]{2,1,0:T(8,128)S(1)}, u32[]{:S(2)}, u32[]{:S(2)}) async-start(f32[8,48,256]{2,1,0:T(8,128)} %bitcast.5), calls=%async_computation.1 | async-start | bytes 786432 | tf_op jit(solution)/shard_map/all_to_all | solution.py:247
  45.7 13.1 %copy-start.1 = (f32[15,512]{1,0:T(8,128)S(1)}, f32[15,512]{1,0:T(8,128)}, u32[]{:S(2)}) copy-start(f32[15,512]{1,0:T(8,128)} %param.25) | copy-start | bytes 92164
  45.7 21.7 %copy-start.2 = (f32[16,32]{1,0:T(8,128)S(1)}, f32[16,32]{1,0:T(8,128)}, u32[]{:S(2)}) copy-start(f32[16,32]{1,0:T(8,128)} %constant.50.clone) | copy-start | bytes 6148
  52.8 13.2 %all-to-all-start.2 = ((f32[32,1,240]{2,1,0:T(1,128)}), f32[32,1,240]{2,1,0:T(1,128)S(1)}, u32[]{:S(2)}, u32[]{:S(2)}) async-start(f32[32,1,240]{2,1,0:T(1,128)} %reshape.244), calls=%async_computation.2 | async-start | bytes 65536 | tf_op jit(solution)/shard_map/all_to_all | solution.py:256
where the time goes:
time: 69.7 us; the launch traced here: 69 us
  Pallas kernels  23.3 us (33%)
  starting transfers between devices  19.2 us (28%)
  local copies, waits for them, and re-layouts  13.1 us (19%)
  waiting for transfers between devices  5.66 us (8%)
  matrix products  4.09 us (6%)
  other arithmetic  2.85 us (4%)
  between operations  0.78 us (1%)
    pallas_call x1, Pallas kernels, fit(): pl.pallas_call(fit_kernel, grid=(steps,), in_specs=[pl.BlockSpec(memory_s...  11.5 us
    all_to_all x1, starting transfers between devices, body(): lax.all_to_all(sent, 'dev', split_axis=0, concat_axis=0, tiled=True)  7.31 us
    pallas_call x1, Pallas kernels, pair_table(): pl.pallas_call(pair_kernel, grid=(steps,), in_specs=[pl.BlockSpec((block,...  6.53 us
    all_to_all x1, starting transfers between devices, body(): lax.all_to_all(spread, ('grp', 'dev'), split_axis=0, concat_axis=0, tiled...  6 us
    all_to_all x1, starting transfers between devices, body(): lax.all_to_all(answers, 'dev', split_axis=0, concat_axis=0, tiled=True)  5.92 us
    all_to_all x1, waiting for transfers between devices, body(): lax.all_to_all(spread, ('grp', 'dev'), split_axis=0, concat_axis=0, tiled...  5.58 us
    pallas_call x1, Pallas kernels, fields(): pl.pallas_call(field_kernel, out_shape=[jax.ShapeDtypeStruct((number, KEE...  5.3 us
    gather x1, local copies, waits for them, and re-layouts, body(): answers = pairs[wanted].reshape(devices, capacity, KEEP * KEEP)  3.7 us
  transfers between devices with their start and end apart: 3, of which 2 were waited for; matrix products, arithmetic and copies ran while one was open for 6% of the time, Pallas kernels for 26%

commit v1 on v0

v1 whole, which is shorter than its diff:
```python
import functools

import jax
import jax.numpy as jnp
import numpy as np
from jax import lax
from jax.experimental import pallas as pl
from jax.experimental.pallas import tpu as pltpu
from jax.sharding import PartitionSpec as P

G = 32
KEEP = 16
S = 16
AREA = KEEP * KEEP
HALF = G // 2
LANES = 128
FITS = 4
CHUNKS = 8
MESH = pl.DeviceIdType.MESH
f32 = jnp.float32
bf16 = jnp.bfloat16
highest = lax.Precision.HIGHEST


def np_tables():
    orders = np.arange(KEEP, dtype=np.float64)
    points = np.arange(G, dtype=np.float64) + 0.5
    cosines = np.cos(np.pi * orders[:, None] * points[None, :] / G)
    weights = np.where(orders == 0, 1.0, 2.0) / G
    return cosines, weights[:, None] * cosines


COS, FIT = np_tables()


def split_np(values):
    values = np.asarray(values, np.float32)
    high = values.astype(jnp.bfloat16)
    return high, (values - high.astype(np.float32)).astype(jnp.bfloat16)


INNER = np.einsum("dh,el->dehl", FIT, FIT).reshape(AREA, G * G)
WEIGHTS = np.concatenate(split_np(INNER), axis=0)
SMALL = np.concatenate([np.repeat(COS, S, axis=1), FIT, np.zeros((KEEP, LANES - G))], axis=1).astype(np.float32)


def round_up(value, step):
    return -(-value // step) * step


def iota(shape, axis):
    return lax.broadcasted_iota(jnp.int32, shape, axis)


def nn(a, b, precision=None):
    return lax.dot_general(a, b, (((1,), (0,)), ((), ())), precision=precision, preferred_element_type=f32)


def nt(a, b, precision=None):
    return lax.dot_general(a, b, (((1,), (1,)), ((), ())), precision=precision, preferred_element_type=f32)


def tn(a, b, precision=None):
    return lax.dot_general(a, b, (((0,), (0,)), ((), ())), precision=precision, preferred_element_type=f32)


def split(values):
    high = values.astype(bf16)
    return high, (values - high.astype(f32)).astype(bf16)


def ones_at(mask):
    return jnp.where(mask, 1.0, 0.0).astype(bf16)


def total(values, axis):
    return jnp.sum(values, axis=axis, keepdims=True)


def fit_orders(s, d):
    u = [s[j] + s[15 - j] for j in range(8)]
    v = [s[j] - s[15 - j] for j in range(8)]
    uu = [u[j] + u[7 - j] for j in range(4)]
    uv = [u[j] - u[7 - j] for j in range(4)]
    out = []
    for c in range(KEEP):
        if c % 2:
            terms = d
        elif c % 4:
            terms = v
        elif c % 8:
            terms = uv
        else:
            terms = uu
        acc = float(FIT[c, 0]) * terms[0]
        for j in range(1, len(terms)):
            acc = acc + float(FIT[c, j]) * terms[j]
        out.append(acc)
    return out


def kernel(
    energies, triples, surfaces, pair_slot, singles, modals, mode_slot, weights_hbm, small,
    coefficients, energy_out, mean_out,
    values, surf, weights, planes, acc, table, hits, answers, arrived, pair_t, padded, message, received,
    modes_in, exp_modals, deep, moved, moments,
    load_sem, send_msg, recv_msg, send_ans, recv_ans, send_mom, recv_mom,
    *, devices, groups,
):
    number = triples.shape[0]
    needs = 3 * number
    pair_rows = surfaces.shape[0]
    mode_rows = modals.shape[0]
    modes = pair_slot.shape[0]
    capacity = needs // devices
    cap = answers.shape[1]
    slots = devices * cap
    bands = -(-mode_rows // 8)
    offset = 2 * KEEP * bands
    width = moved.shape[2]
    everyone = devices * groups
    me = lax.axis_index("dev")
    group = lax.axis_index("grp")
    flat = group * devices + me

    loads = [pltpu.make_async_copy(weights_hbm, weights, load_sem.at[0])]
    loads.append(pltpu.make_async_copy(surfaces, surf, load_sem.at[1]))
    part = energies.shape[1] // CHUNKS
    for i in range(CHUNKS):
        span = pl.ds(i * part, part)
        loads.append(pltpu.make_async_copy(energies.at[:, span], values.at[:, span], load_sem.at[2 + i]))
    for load in loads:
        load.start()

    barrier = pltpu.get_barrier_semaphore()

    def greet(k, carry):
        other = lax.rem(flat + k, everyone)
        pl.semaphore_signal(
            barrier, inc=1, device_id=(other // devices, lax.rem(other, devices)), device_id_type=MESH
        )
        return carry

    lax.fori_loop(1, everyone, greet, 0)

    padded[...] = jnp.zeros_like(padded)
    padded[0, :number, 0:3] = triples[...].astype(f32)
    padded[1, 0:modes, 0:modes] = pair_slot[...].astype(f32)
    padded[2, 0:1, 0:modes] = mode_slot[...].astype(f32)
    turned = padded[0].T
    picks = [turned[p : p + 1, :].astype(jnp.int32) for p in range(3)]
    rows = iota((LANES, number), 0)
    on = [rows == pick for pick in picks]
    on_hot = [ones_at(x) for x in on]
    pair_ints = padded[1].astype(jnp.int32)
    first_two = jnp.concatenate(on_hot[:2], axis=1)
    lines = 128.0 * nn((pair_ints >> 7).astype(f32).astype(bf16), first_two)
    lines = lines + nn((pair_ints & 127).astype(f32).astype(bf16), first_two)
    chosen = [
        total(jnp.where(on[1], lines[:, :number], 0.0), 0),
        total(jnp.where(on[2], lines[:, :number], 0.0), 0),
        total(jnp.where(on[2], lines[:, number:], 0.0), 0),
    ]
    flips = [picks[0] > picks[1], picks[0] > picks[2], picks[1] > picks[2]]
    pair_ids = (jnp.concatenate(chosen, axis=1) + 0.5).astype(jnp.int32)
    holders = iota((devices, needs), 0)
    held = (pair_ids >= holders * pair_rows) & (pair_ids < (holders + 1) * pair_rows)
    held_hot = ones_at(held)
    owner = total(jnp.where(held, holders, 0), 0)
    local = pair_ids - owner * pair_rows
    before = ones_at(iota((number, number), 0) < iota((number, number), 1))
    seen = jnp.zeros((devices, 1), f32)
    ranks = []
    for p in range(3):
        block = held_hot[:, p * number : (p + 1) * number]
        mine = held[:, p * number : (p + 1) * number]
        ranks.append(total(jnp.where(mine, nn(block, before) + seen, 0.0), 0))
        seen = seen + total(jnp.where(mine, 1.0, 0.0), 1)
    rank = (jnp.concatenate(ranks, axis=1) + 0.5).astype(jnp.int32)
    place = owner * cap + rank
    at_rank = ones_at(iota((LANES, needs), 0) == rank)
    coarse = jnp.where(held, (local >> 4).astype(f32), 0.0).astype(bf16)
    fine = jnp.where(held, (local & 15).astype(f32), 0.0).astype(bf16)
    requests = 16.0 * nt(coarse, at_rank) + nt(fine, at_rank)

    modes_in[...] = jnp.zeros_like(modes_in)
    modes_in[0:mode_rows, 0 : G * S] = modals[...]
    modes_in[0:mode_rows, G * S : G * S + G] = singles[...]
    every = modes_in[:, 0 : G * S]
    spread = small[:, 0 : G * S]
    lane = iota((KEEP, G * S), 1)
    ground_weights = jnp.where((lane & (S - 1)) == 0, spread, 0.0)
    ground_here = nt(every * every, ground_weights, highest)
    single_here = nt(modes_in[:, G * S : G * S + G], small[:, G * S : G * S + G], highest)
    padded[3, 0 : modes_in.shape[0], 0:KEEP] = ground_here
    padded[3, 0 : modes_in.shape[0], KEEP : 2 * KEEP] = single_here
    base = padded[3, 0:8, :]
    for q in range(1, bands):
        base = base + pltpu.roll(padded[3, 8 * q : 8 * q + 8, :], 2 * KEEP * q, 1)
    asked = pltpu.roll(requests, offset, 1)
    top = iota((8, LANES), 0) == 0
    for p in range(devices):
        message[p] = base + jnp.where(top, asked[p : p + 1, :], 0.0)
    received[me] = message[me]

    pl.semaphore_wait(barrier, everyone - 1)

    def message_copy(peer, slot):
        return pltpu.make_async_remote_copy(
            src_ref=message.at[peer], dst_ref=received.at[slot],
            send_sem=send_msg.at[peer], recv_sem=recv_msg.at[slot],
            device_id=(group, peer), device_id_type=MESH,
        )

    def answer_copy(peer, slot):
        return pltpu.make_async_remote_copy(
            src_ref=answers.at[peer], dst_ref=arrived.at[slot],
            send_sem=send_ans.at[peer], recv_sem=recv_ans.at[slot],
            device_id=(group, peer), device_id_type=MESH,
        )

    def each_peer(action):
        def step(k, carry):
            action(lax.rem(me + k, devices))
            return carry

        lax.fori_loop(1, devices, step, 0)

    each_peer(lambda peer: message_copy(peer, me).start())

    loads[0].wait()
    loads[1].wait()
    w_high = weights[0:AREA, :]
    w_low = weights[AREA : 2 * AREA, :]
    table_rows = table.shape[1]
    done = 0
    while done < table_rows:
        size = min(256, table_rows - done)
        have = min(size, pair_rows - done)
        whole = have // 16 * 16
        pieces = []
        if whole:
            pieces.append(surf[done : done + whole, :])
        if size > whole:
            rest = jnp.zeros((size - whole, G * G), f32)
            if have > whole:
                tail = jnp.concatenate(
                    [surf[done + whole : done + have, :], jnp.zeros((16 - (have - whole), G * G), f32)], axis=0
                )
                pieces.append(tail)
                rest = jnp.zeros((size - whole - 16, G * G), f32)
            if rest.shape[0]:
                pieces.append(None)
        at = done
        for piece in pieces:
            if piece is None:
                table[:, at : done + size, :] = jnp.zeros((2, done + size - at, AREA), bf16)
                continue
            high, low = split(piece)
            fitted = nt(high, w_high) + nt(high, w_low) + nt(low, w_high)
            count = piece.shape[0]
            part_high, part_low = split(fitted)
            table[0, at : at + count, :] = part_high
            table[1, at : at + count, :] = part_low
            at += count
        done += size

    each_peer(lambda peer: message_copy(me, peer).wait_recv())
    wanted = jnp.concatenate([received[p, 0:1, :] for p in range(devices)], axis=0)
    wanted = jnp.concatenate([wanted, jnp.zeros((LANES - devices, LANES), f32)], axis=0)
    wanted = (wanted.T[offset : offset + cap if offset + cap <= LANES else LANES, :] + 0.5).astype(jnp.int32)
    in_table = iota((capacity, table_rows), 1)
    if cap > capacity:
        hits[...] = jnp.zeros_like(hits)
    for p in range(devices):
        hits[p, 0:capacity, :] = ones_at(wanted[0:capacity, p : p + 1] == in_table)
    all_hits = hits[...].reshape(slots, table_rows)
    found = nn(all_hits, table[0]) + nn(all_hits, table[1])
    answers[...] = found.reshape(devices, cap, AREA)
    arrived[me] = answers[me]
    each_peer(lambda peer: answer_copy(peer, me).start())

    modes_hot = jnp.concatenate(on_hot, axis=1)
    slot_ids = (nn(padded[2, 0:8, :].astype(bf16), modes_hot)[0:1, :] + 0.5).astype(jnp.int32)
    homes = iota((devices, needs), 0)
    home = (slot_ids >= homes * mode_rows) & (slot_ids < (homes + 1) * mode_rows)
    home_row = total(jnp.where(home, homes, 0), 0)
    at_home = slot_ids - home_row * mode_rows
    spot = home_row * 8 + (at_home & 7)
    spot_hot = ones_at(iota((devices * 8, needs), 0) == spot)
    tables_high, tables_low = split(received[...].reshape(devices * 8, LANES))
    looked = tn(tables_high, spot_hot) + tn(tables_low, spot_hot)
    band = at_home >> 3
    taken = jnp.where(band == 0, looked[0 : 2 * KEEP], 0.0)
    for q in range(1, bands):
        taken = jnp.where(band == q, looked[2 * KEEP * q : 2 * KEEP * (q + 1)], taken)
    ground = [taken[0:KEEP, p * number : (p + 1) * number] for p in range(3)]
    single = [taken[KEEP : 2 * KEEP, p * number : (p + 1) * number] for p in range(3)]

    for load in loads[2:]:
        load.wait()

    def fit_step(step, carry):
        for i in range(FITS):
            j = step * FITS + i
            front = values[:, pl.ds(pl.multiple_of(j * G * G, G * G), G * G)]
            back = values[:, pl.ds(pl.multiple_of((G - 1 - j) * G * G, G * G), G * G)]
            both = jnp.concatenate([front, back], axis=0)
            plane = nt(weights[0:AREA, :], both) + nt(weights[AREA : 2 * AREA, :], both)
            planes[j] = plane[:, :number] + plane[:, number:]
            planes[HALF + j] = plane[:, :number] - plane[:, number:]
        return carry

    lax.fori_loop(0, HALF // FITS, fit_step, 0)

    def order_step(step, carry):
        span = pl.ds(pl.multiple_of(step * 8, 8), 8)
        sums = [planes[j, span, :] for j in range(HALF)]
        differences = [planes[HALF + j, span, :] for j in range(HALF)]
        for c, value in enumerate(fit_orders(sums, differences)):
            acc[c, span, :] = value
        return carry

    lax.fori_loop(0, AREA // 8, order_step, 0)

    rows16 = modes_in.shape[0]
    for g in range(G):
        exp_modals[g * rows16 : (g + 1) * rows16, 0:S] = modes_in[:, g * S : (g + 1) * S]
    pieces = exp_modals[:, 0:S]
    columns = iota((S, AREA), 1)
    index = iota((S, AREA), 0)
    by_a = jnp.where((columns >> 4) == index, 1.0, 0.0)
    by_b = jnp.where((columns & (S - 1)) == index, 1.0, 0.0)
    products = nn(pieces, by_a, highest) * nn(pieces, by_b, highest)
    tall = jnp.concatenate([spread] * (width // KEEP), axis=0)
    own_row = (iota(tall.shape, 1) & (rows16 - 1)) == (iota(tall.shape, 0) >> 4)
    deep[...] = nn(jnp.where(own_row, tall, 0.0), products, highest)

    each_peer(lambda peer: answer_copy(me, peer).wait_recv())
    place_hot = ones_at(iota((slots, needs), 0) == place)
    arrived_high, arrived_low = split(arrived[...].reshape(slots, AREA))
    ordered = tn(arrived_high, place_hot) + tn(arrived_low, place_hot)
    for p in range(3):
        pair_t[p] = ordered[:, p * number : (p + 1) * number]

    def pair_rows_of(p, c):
        straight = pair_t[p, c * KEEP : (c + 1) * KEEP, :]
        turned_rows = pair_t[p, pl.ds(c, KEEP, stride=KEEP), :]
        return jnp.where(flips[p], turned_rows, straight)

    first_row = iota((KEEP, number), 0) == 0
    for c in range(KEEP):
        along_d = pair_rows_of(0, c)
        along_e = pair_rows_of(1, c) + jnp.where(first_row, single[0][c : c + 1, :], 0.0)
        if c == 0:
            along_d = along_d + single[1]
            along_e = along_e + single[2]
            for d in range(KEEP):
                acc[0, d * KEEP : (d + 1) * KEEP, :] -= pair_rows_of(2, d)
        acc[c, pl.ds(0, KEEP, stride=KEEP), :] -= along_d
        acc[c, 0:KEEP, :] -= along_e

    low3, high3 = ground[2][0:8], ground[2][8:16]
    rows1 = [ground[0][c : c + 1, :] for c in range(KEEP)]
    partial1 = [jnp.zeros((8, number), f32) for _ in range(KEEP)]
    field2 = []
    field3 = [jnp.zeros((8, number), f32) for _ in range(2)]
    for d in range(KEEP):
        row2 = ground[1][d : d + 1, :]
        inner = jnp.zeros((8, number), f32)
        for h, part3 in enumerate((low3, high3)):
            weight = row2 * part3
            mixed = jnp.zeros((8, number), f32)
            for c in range(KEEP):
                value = acc[c, d * KEEP + 8 * h : d * KEEP + 8 * h + 8, :]
                partial1[c] = partial1[c] + value * weight
                mixed = mixed + value * rows1[c]
            inner = inner + mixed * part3
            field3[h] = field3[h] + mixed * row2
        field2.append(total(inner, 0))
    field1 = jnp.concatenate([total(x, 0) for x in partial1], axis=0)
    field2 = jnp.concatenate(field2, axis=0)
    field3 = jnp.concatenate(field3, axis=0)
    energy_out[...] = total(field1 * ground[0], 0)

    fields = jnp.concatenate([field1, field2, field3], axis=1)
    fields = jnp.concatenate([fields] * (width // KEEP), axis=0)
    of_row = (iota((width, needs), 0) >> 4) == at_home
    fields_high, fields_low = split(jnp.where(of_row, fields, 0.0))
    home_hot = ones_at(home)
    sums = nt(home_hot, fields_high) + nt(home_hot, fields_low)
    for p in range(devices):
        moved[p] = sums[p : p + 1, :]
    moments[flat] = moved[me]

    def moment_copy(other, owner_dev, slot):
        return pltpu.make_async_remote_copy(
            src_ref=moved.at[owner_dev], dst_ref=moments.at[slot],
            send_sem=send_mom.at[other], recv_sem=recv_mom.at[slot],
            device_id=(other // devices, lax.rem(other, devices)), device_id_type=MESH,
        )

    def each_other(action):
        def step(k, carry):
            action(lax.rem(flat + k, everyone))
            return carry

        lax.fori_loop(1, everyone, step, 0)

    each_other(lambda other: moment_copy(other, lax.rem(other, devices), flat).start())

    for c in range(KEEP):
        coefficients[:, c * AREA : (c + 1) * AREA] = acc[c].T.astype(bf16)

    each_other(lambda other: moment_copy(flat, me, other).wait_recv())
    summed = moments[0]
    for k in range(1, everyone):
        summed = summed + moments[k]
    chosen_rows = (iota((rows16, width), 1) >> 4) == iota((rows16, width), 0)
    mean = nn(jnp.where(chosen_rows, summed, 0.0), deep[...], highest)
    mean_out[...] = mean[0:mode_rows, :]

    each_peer(lambda peer: message_copy(peer, me).wait_send())
    each_peer(lambda peer: answer_copy(peer, me).wait_send())
    each_other(lambda other: moment_copy(other, lax.rem(other, devices), flat).wait_send())


def body(energies, triples, pair_surfaces, pair_slot, single_surfaces, modals, mode_slot):
    devices = lax.axis_size("dev")
    groups = lax.axis_size("grp")
    number = triples.shape[0]
    pair_rows = pair_surfaces.shape[0]
    mode_rows = modals.shape[0]
    cap = round_up(3 * number // devices, 16)
    table_rows = round_up(pair_rows, 256)
    width = round_up(mode_rows * KEEP, LANES)
    rows16 = 16
    everyone = devices * groups
    vmem = pl.BlockSpec(memory_space=pltpu.VMEM)
    anywhere = pl.BlockSpec(memory_space=pl.ANY)
    coefficients, energy, mean = pl.pallas_call(
        functools.partial(kernel, devices=devices, groups=groups),
        in_specs=[anywhere, vmem, anywhere, vmem, vmem, vmem, vmem, anywhere, vmem],
        out_specs=[vmem, vmem, vmem],
        out_shape=[
            jax.ShapeDtypeStruct((number, KEEP * AREA), bf16),
            jax.ShapeDtypeStruct((1, number), f32),
            jax.ShapeDtypeStruct((mode_rows, S * S), f32),
        ],
        scratch_shapes=[
            pltpu.VMEM(energies.shape, bf16),
            pltpu.VMEM(pair_surfaces.shape, f32),
            pltpu.VMEM(WEIGHTS.shape, bf16),
            pltpu.VMEM((G, AREA, number), f32),
            pltpu.VMEM((KEEP, AREA, number), f32),
            pltpu.VMEM((2, table_rows, AREA), bf16),
            pltpu.VMEM((devices, cap, table_rows), bf16),
            pltpu.VMEM((devices, cap, AREA), f32),
            pltpu.VMEM((devices, cap, AREA), f32),
            pltpu.VMEM((3, AREA, number), f32),
            pltpu.VMEM((4, LANES, LANES), f32),
            pltpu.VMEM((devices, 8, LANES), f32),
            pltpu.VMEM((devices, 8, LANES), f32),
            pltpu.VMEM((rows16, SMALL.shape[1]), f32),
            pltpu.VMEM((G * rows16, LANES), f32),
            pltpu.VMEM((width, AREA), f32),
            pltpu.VMEM((devices, 1, width), f32),
            pltpu.VMEM((everyone, 1, width), f32),
            pltpu.SemaphoreType.DMA((2 + CHUNKS,)),
            pltpu.SemaphoreType.DMA((devices,)),
            pltpu.SemaphoreType.DMA((devices,)),
            pltpu.SemaphoreType.DMA((devices,)),
            pltpu.SemaphoreType.DMA((devices,)),
            pltpu.SemaphoreType.DMA((everyone,)),
            pltpu.SemaphoreType.DMA((everyone,)),
        ],
        compiler_params=pltpu.CompilerParams(
            collective_id=0, has_side_effects=True, vmem_limit_bytes=60 * 1024 * 1024
        ),
    )(
        energies, triples, pair_surfaces, pair_slot, single_surfaces, modals, mode_slot.reshape(1, -1),
        jnp.asarray(WEIGHTS), jnp.asarray(SMALL),
    )
    return coefficients, energy.reshape(number), mean


def solution(mesh):
    in_specs = (
        P(("grp", "dev"), None),
        P(("grp", "dev"), None),
        P("dev", None),
        P(),
        P("dev", None),
        P("dev", None),
        P(),
    )
    out_specs = (P(("grp", "dev"), None), P(("grp", "dev")), P("dev", None))
    return jax.shard_map(body, mesh=mesh, in_specs=in_specs, out_specs=out_specs, check_vma=False)
```

time: 69.7 us -> 38.8 us (0.56)
  starting transfers between devices: 19.2 us -> 0 us
  Pallas kernels: 23.3 us -> 31.7 us
  local copies, waits for them, and re-layouts: 13.1 us -> 6.16 us
  waiting for transfers between devices: 5.66 us -> 0 us
  matrix products: 4.09 us -> 0 us
  other arithmetic: 2.85 us -> 0 us
    all_to_all x3 -> x0, starting transfers between devices: 19.2 us -> none  [the longest x1 7.31 us: body(): lax.all_to_all(sent, 'dev', split_axis=0, concat_axis=0, tiled=True)]
    pallas_call x3 -> x1, Pallas kernels: 23.3 us -> 31.7 us  [body(): pl.pallas_call(functools.partial(kernel, devices=devices, groups=groups),...]
    gather x2 -> x0, local copies, waits for them, and re-layouts: 5.87 us -> none  [the longest x1 3.7 us: body(): answers = pairs[wanted].reshape(devices, capacity, KEEP * KEEP)]
    all_to_all x3 -> x0, waiting for transfers between devices: 5.66 us -> none  [the longest x1 5.58 us: body(): lax.all_to_all(spread, ('grp', 'dev'), split_axis=0, concat_axis=0, tiled...]
    unnamed x11 -> x4, local copies, waits for them, and re-layouts: 0.9 us -> 6.16 us
    dot_general x5 -> x0, matrix products: 4.09 us -> none  [the longest x1 1.22 us: body(): jnp.dot((lower[:, None] == mode_ids[None, :]).astype(jnp.float32), pair_s...]
    broadcast_in_dim x5 -> x0, local copies, waits for them, and re-layouts: 2.29 us -> none  [the longest x2 0.86 us: body(): jnp.broadcast_to(partial.reshape(1, devices, mode_rows, KEEP), (groups, d...]
    reshape x6 -> x0, local copies, waits for them, and re-layouts: 1.79 us -> none  [the longest x1 0.72 us: body(): mean_field.reshape(mode_rows, S * S)]
  transfers between devices with their start and end apart: 3 -> 0, of which waited for: 2 -> 0; matrix products, arithmetic and copies ran while one was open for 6% -> 0% of each run, Pallas kernels for 26% -> 0%
where the time goes in v1:
time: 38.8 us; the launch traced here: 38.5 us
  Pallas kernels  31.7 us (82%)
  local copies, waits for them, and re-layouts  6.16 us (16%)
  between operations  0.64 us (2%)
    pallas_call x1, Pallas kernels, body(): pl.pallas_call(functools.partial(kernel, devices=devices, groups=groups),...  31.7 us
    unnamed x4, local copies, waits for them, and re-layouts  6.16 us

profile of v1, /device:TPU:0, one launch (start us, length us, event | category | flops | bytes accessed | tf_op | source)
XLA Modules:
  0.0 38.5 jit_solution(7344872493912812687)
XLA Ops:
  0.6 1.4 %copy.12.triples = s32[128,3]{1,0:T(8,128)} copy(s32[128,3]{0,1:T(4,128)} %param.10) | data formatting | bytes 3072 | tf_op args[1]
  2.0 31.7 %shard_map.112 = (bf16[128,4096]{1,0:T(8,128)(2,1)}, f32[1,128]{1,0:T(1,128)}, f32[15,256]{1,0:T(8,128)}) custom-call(bf16[128,32768]{1,0:T(8,128)(2,1)} %energies.1, s32[128,3]{1,0:T(8,128)} %copy.12.triples, f32[900,1024]{1,0:T(8,128)} %surfaces.1, s32[114,114]{1,0:T(8,128)} %pair_slot.1, f32[15,32]{1,0:T(8,128)} %singles.1, f32[15,512]{1,0:T(8,128)} %modals.1, ...), custom_call_target="tpu_custom_call" | custom-call | tf_op jit(solution)/shard_map/pallas_call | solution.py:441
  33.7 2.3 %copy.16 = bf16[128,4096]{1,0:T(8,128)(2,1)} copy(bf16[128,4096]{1,0:T(8,128)(2,1)} %get-tuple-element.12) | data formatting | bytes 2097152
  36.0 1.1 %copy.17 = f32[128]{0:T(128)} copy(f32[128]{0:T(128)} %bitcast.3) | data formatting | bytes 1024
  37.2 1.3 %copy.18 = f32[15,256]{1,0:T(8,128)} copy(f32[15,256]{1,0:T(8,128)} %get-tuple-element.14) | data formatting | bytes 30720

commit v2 on v1

--- a/solution.py
+++ b/solution.py
@@ -14,8 +14,10 @@
 AREA = KEEP * KEEP
 HALF = G // 2
 LANES = 128
-FITS = 4
+STEPS = 4
+EARLY = 1
 CHUNKS = 8
+SMALLS = 6
 MESH = pl.DeviceIdType.MESH
 f32 = jnp.float32
 bf16 = jnp.bfloat16
@@ -77,41 +79,45 @@
     return jnp.sum(values, axis=axis, keepdims=True)
 
 
-def fit_orders(s, d):
-    u = [s[j] + s[15 - j] for j in range(8)]
-    v = [s[j] - s[15 - j] for j in range(8)]
-    uu = [u[j] + u[7 - j] for j in range(4)]
-    uv = [u[j] - u[7 - j] for j in range(4)]
+def members(step):
+    return step, 15 - step, 7 - step, 8 + step
+
+
+def fit_orders(step, s, d):
+    js = members(step)
+    u, v = (s[0] + s[1], s[2] + s[3]), (s[0] - s[1], s[2] - s[3])
     out = []
     for c in range(KEEP):
         if c % 2:
-            terms = d
+            terms = list(zip(js, d))
         elif c % 4:
-            terms = v
+            terms = [(js[0], v[0]), (js[2], v[1])]
         elif c % 8:
-            terms = uv
+            terms = [(js[0], u[0] - u[1])]
         else:
-            terms = uu
-        acc = float(FIT[c, 0]) * terms[0]
-        for j in range(1, len(terms)):
-            acc = acc + float(FIT[c, j]) * terms[j]
-        out.append(acc)
+            terms = [(js[0], u[0] + u[1])]
+        value = None
+        for j, term in terms:
+            scaled = float(FIT[c, j]) * term
+            value = scaled if value is None else value + scaled
+        out.append(value)
     return out
 
 
 def kernel(
-    energies, triples, surfaces, pair_slot, singles, modals, mode_slot, weights_hbm, small,
+    energies, triples_hbm, surfaces, pair_slot_hbm, singles_hbm, modals_hbm, mode_slot_hbm, weights_hbm, small_hbm,
     coefficients, energy_out, mean_out,
+    triples, pair_slot, singles, modals, mode_slot, small,
     values, surf, weights, planes, acc, table, hits, answers, arrived, pair_t, padded, message, received,
     modes_in, exp_modals, deep, moved, moments,
     load_sem, send_msg, recv_msg, send_ans, recv_ans, send_mom, recv_mom,
     *, devices, groups,
 ):
-    number = triples.shape[0]
+    number = triples_hbm.shape[1]
     needs = 3 * number
     pair_rows = surfaces.shape[0]
-    mode_rows = modals.shape[0]
-    modes = pair_slot.shape[0]
+    mode_rows = modals_hbm.shape[0]
+    modes = pair_slot_hbm.shape[0]
     capacity = needs // devices
     cap = answers.shape[1]
     slots = devices * cap
@@ -123,32 +129,47 @@
     group = lax.axis_index("grp")
     flat = group * devices + me
 
-    loads = [pltpu.make_async_copy(weights_hbm, weights, load_sem.at[0])]
-    loads.append(pltpu.make_async_copy(surfaces, surf, load_sem.at[1]))
+    pairs = [
+        (triples_hbm, triples), (pair_slot_hbm, pair_slot), (singles_hbm, singles),
+        (modals_hbm, modals), (mode_slot_hbm, mode_slot), (small_hbm, small),
+        (weights_hbm, weights), (surfaces, surf),
+    ]
     part = energies.shape[1] // CHUNKS
     for i in range(CHUNKS):
         span = pl.ds(i * part, part)
-        loads.append(pltpu.make_async_copy(energies.at[:, span], values.at[:, span], load_sem.at[2 + i]))
-    for load in loads:
+        pairs.append((energies.at[:, span], values.at[:, span]))
+    loads = [pltpu.make_async_copy(source, target, load_sem.at[i]) for i, (source, target) in enumerate(pairs)]
+    for load in loads[:SMALLS]:
         load.start()
 
     barrier = pltpu.get_barrier_semaphore()
 
-    def greet(k, carry):
-        other = lax.rem(flat + k, everyone)
-        pl.semaphore_signal(
-            barrier, inc=1, device_id=(other // devices, lax.rem(other, devices)), device_id_type=MESH
-        )
-        return carry
-
-    lax.fori_loop(1, everyone, greet, 0)
+    def each_peer(action):
+        def step(k, carry):
+            action(lax.rem(me + k, devices))
+            return carry
+
+        lax.fori_loop(1, devices, step, 0)
+
+    def each_other(action):
+        each_peer(lambda peer: action(group, peer))
+        for k in range(1, groups):
+            there = lax.rem(group + k, groups)
+            action(there, me)
+            each_peer(lambda peer: action(there, peer))
+
+    each_other(
+        lambda there, peer: pl.semaphore_signal(barrier, inc=1, device_id=(there, peer), device_id_type=MESH)
+    )
+    for load in loads[SMALLS:]:
+        load.start()
+    for load in loads[:SMALLS]:
+        load.wait()
 
     padded[...] = jnp.zeros_like(padded)
-    padded[0, :number, 0:3] = triples[...].astype(f32)
     padded[1, 0:modes, 0:modes] = pair_slot[...].astype(f32)
     padded[2, 0:1, 0:modes] = mode_slot[...].astype(f32)
-    turned = padded[0].T
-    picks = [turned[p : p + 1, :].astype(jnp.int32) for p in range(3)]
+    picks = [triples[p : p + 1, :] for p in range(3)]
     rows = iota((LANES, number), 0)
     on = [rows == pick for pick in picks]
     on_hot = [ones_at(x) for x in on]
@@ -219,17 +240,10 @@
             device_id=(group, peer), device_id_type=MESH,
         )
 
-    def each_peer(action):
-        def step(k, carry):
-            action(lax.rem(me + k, devices))
-            return carry
-
-        lax.fori_loop(1, devices, step, 0)
-
     each_peer(lambda peer: message_copy(peer, me).start())
 
-    loads[0].wait()
-    loads[1].wait()
+    loads[SMALLS].wait()
+    loads[SMALLS + 1].wait()
     w_high = weights[0:AREA, :]
     w_low = weights[AREA : 2 * AREA, :]
     table_rows = table.shape[1]
@@ -265,6 +279,31 @@
             at += count
         done += size
 
+    for load in loads[SMALLS + 2 :]:
+        load.wait()
+
+    def inner_fit(step):
+        for i, j in enumerate(members(step)):
+            front = values[:, j * G * G : (j + 1) * G * G]
+            back = values[:, (G - 1 - j) * G * G : (G - j) * G * G]
+            both = jnp.concatenate([front, back], axis=0)
+            plane = nt(weights[0:AREA, :], both) + nt(weights[AREA : 2 * AREA, :], both)
+            planes[step % 2, i] = plane[:, :number] + plane[:, number:]
+            planes[step % 2, 4 + i] = plane[:, :number] - plane[:, number:]
+
+    def outer_fit(step):
+        for block in range(AREA // 8):
+            span = slice(block * 8, block * 8 + 8)
+            sums = [planes[step % 2, i, span, :] for i in range(4)]
+            differences = [planes[step % 2, 4 + i, span, :] for i in range(4)]
+            for c, value in enumerate(fit_orders(step, sums, differences)):
+                acc[c, span, :] = value if step == 0 else acc[c, span, :] + value
+
+    for step in range(EARLY):
+        inner_fit(step)
+        if step:
+            outer_fit(step - 1)
+
     each_peer(lambda peer: message_copy(me, peer).wait_recv())
     wanted = jnp.concatenate([received[p, 0:1, :] for p in range(devices)], axis=0)
     wanted = jnp.concatenate([wanted, jnp.zeros((LANES - devices, LANES), f32)], axis=0)
@@ -297,44 +336,10 @@
     ground = [taken[0:KEEP, p * number : (p + 1) * number] for p in range(3)]
     single = [taken[KEEP : 2 * KEEP, p * number : (p + 1) * number] for p in range(3)]
 
-    for load in loads[2:]:
-        load.wait()
-
-    def fit_step(step, carry):
-        for i in range(FITS):
-            j = step * FITS + i
-            front = values[:, pl.ds(pl.multiple_of(j * G * G, G * G), G * G)]
-            back = values[:, pl.ds(pl.multiple_of((G - 1 - j) * G * G, G * G), G * G)]
-            both = jnp.concatenate([front, back], axis=0)
-            plane = nt(weights[0:AREA, :], both) + nt(weights[AREA : 2 * AREA, :], both)
-            planes[j] = plane[:, :number] + plane[:, number:]
-            planes[HALF + j] = plane[:, :number] - plane[:, number:]
-        return carry
-
-    lax.fori_loop(0, HALF // FITS, fit_step, 0)
-
-    def order_step(step, carry):
-        span = pl.ds(pl.multiple_of(step * 8, 8), 8)
-        sums = [planes[j, span, :] for j in range(HALF)]
-        differences = [planes[HALF + j, span, :] for j in range(HALF)]
-        for c, value in enumerate(fit_orders(sums, differences)):
-            acc[c, span, :] = value
-        return carry
-
-    lax.fori_loop(0, AREA // 8, order_step, 0)
-
-    rows16 = modes_in.shape[0]
-    for g in range(G):
-        exp_modals[g * rows16 : (g + 1) * rows16, 0:S] = modes_in[:, g * S : (g + 1) * S]
-    pieces = exp_modals[:, 0:S]
-    columns = iota((S, AREA), 1)
-    index = iota((S, AREA), 0)
-    by_a = jnp.where((columns >> 4) == index, 1.0, 0.0)
-    by_b = jnp.where((columns & (S - 1)) == index, 1.0, 0.0)
-    products = nn(pieces, by_a, highest) * nn(pieces, by_b, highest)
-    tall = jnp.concatenate([spread] * (width // KEEP), axis=0)
-    own_row = (iota(tall.shape, 1) & (rows16 - 1)) == (iota(tall.shape, 0) >> 4)
-    deep[...] = nn(jnp.where(own_row, tall, 0.0), products, highest)
+    for step in range(EARLY, STEPS):
+        inner_fit(step)
+        outer_fit(step - 1)
+    outer_fit(STEPS - 1)
 
     each_peer(lambda peer: answer_copy(me, peer).wait_recv())
     place_hot = ones_at(iota((slots, needs), 0) == place)
@@ -393,26 +398,36 @@
         moved[p] = sums[p : p + 1, :]
     moments[flat] = moved[me]
 
-    def moment_copy(other, owner_dev, slot):
+    def moment_copy(there, peer, slot):
         return pltpu.make_async_remote_copy(
-            src_ref=moved.at[owner_dev], dst_ref=moments.at[slot],
-            send_sem=send_mom.at[other], recv_sem=recv_mom.at[slot],
-            device_id=(other // devices, lax.rem(other, devices)), device_id_type=MESH,
+            src_ref=moved.at[peer], dst_ref=moments.at[slot],
+            send_sem=send_mom.at[there * devices + peer], recv_sem=recv_mom.at[slot],
+            device_id=(there, peer), device_id_type=MESH,
         )
 
-    def each_other(action):
-        def step(k, carry):
-            action(lax.rem(flat + k, everyone))
-            return carry
-
-        lax.fori_loop(1, everyone, step, 0)
-
-    each_other(lambda other: moment_copy(other, lax.rem(other, devices), flat).start())
+    each_other(lambda there, peer: moment_copy(there, peer, flat).start())
 
     for c in range(KEEP):
         coefficients[:, c * AREA : (c + 1) * AREA] = acc[c].T.astype(bf16)
 
-    each_other(lambda other: moment_copy(flat, me, other).wait_recv())
+    rows16 = modes_in.shape[0]
+    for g in range(G):
+        exp_modals[g * rows16 : (g + 1) * rows16, 0:S] = modes_in[:, g * S : (g + 1) * S]
+    pieces = exp_modals[:, 0:S]
+    columns = iota((S, AREA), 1)
+    index = iota((S, AREA), 0)
+    by_a = jnp.where((columns >> 4) == index, 1.0, 0.0)
+    by_b = jnp.where((columns & (S - 1)) == index, 1.0, 0.0)
+    piece_high, piece_low = split(pieces)
+    by_a, by_b = by_a.astype(bf16), by_b.astype(bf16)
+    products = (nn(piece_high, by_a) + nn(piece_low, by_a)) * (nn(piece_high, by_b) + nn(piece_low, by_b))
+    products_high, products_low = split(products)
+    tall = jnp.concatenate([spread] * (width // KEEP), axis=0)
+    own_row = (iota(tall.shape, 1) & (rows16 - 1)) == (iota(tall.shape, 0) >> 4)
+    tall_high, tall_low = split(jnp.where(own_row, tall, 0.0))
+    deep[...] = nn(tall_high, products_high) + nn(tall_high, products_low) + nn(tall_low, products_high)
+
+    each_other(lambda there, peer: moment_copy(group, me, there * devices + peer).wait_recv())
     summed = moments[0]
     for k in range(1, everyone):
         summed = summed + moments[k]
@@ -422,7 +437,20 @@
 
     each_peer(lambda peer: message_copy(peer, me).wait_send())
     each_peer(lambda peer: answer_copy(peer, me).wait_send())
-    each_other(lambda other: moment_copy(other, lax.rem(other, devices), flat).wait_send())
+    each_other(lambda there, peer: moment_copy(there, peer, flat).wait_send())
+
+
+def write_kernel(coefficients, energy, mean, coefficients_out, energy_out, mean_out, sems):
+    copies = [
+        pltpu.make_async_copy(source, target, sems.at[i])
+        for i, (source, target) in enumerate(
+            [(coefficients, coefficients_out), (energy, energy_out), (mean, mean_out)]
+        )
+    ]
+    for copy in copies:
+        copy.start()
+    for copy in copies:
+        copy.wait()
 
 
 def body(energies, triples, pair_surfaces, pair_slot, single_surfaces, modals, mode_slot):
@@ -437,21 +465,27 @@
     rows16 = 16
     everyone = devices * groups
     vmem = pl.BlockSpec(memory_space=pltpu.VMEM)
-    anywhere = pl.BlockSpec(memory_space=pl.ANY)
-    coefficients, energy, mean = pl.pallas_call(
+    hbm = pl.BlockSpec(memory_space=pltpu.HBM)
+    small_shapes = [
+        (triples.shape[::-1], jnp.int32), (pair_slot.shape, jnp.int32), (single_surfaces.shape, f32),
+        (modals.shape, f32), ((1, mode_slot.shape[0]), jnp.int32), (SMALL.shape, f32),
+    ]
+    results = [
+        jax.ShapeDtypeStruct((number, KEEP * AREA), bf16),
+        jax.ShapeDtypeStruct((1, number), f32),
+        jax.ShapeDtypeStruct((mode_rows, S * S), f32),
+    ]
+    in_vmem = pl.pallas_call(
         functools.partial(kernel, devices=devices, groups=groups),
-        in_specs=[anywhere, vmem, anywhere, vmem, vmem, vmem, vmem, anywhere, vmem],
+        in_specs=[hbm] * 9,
         out_specs=[vmem, vmem, vmem],
-        out_shape=[
-            jax.ShapeDtypeStruct((number, KEEP * AREA), bf16),
-            jax.ShapeDtypeStruct((1, number), f32),
-            jax.ShapeDtypeStruct((mode_rows, S * S), f32),
-        ],
+        out_shape=results,
         scratch_shapes=[
+            *[pltpu.VMEM(shape, kind) for shape, kind in small_shapes],
             pltpu.VMEM(energies.shape, bf16),
             pltpu.VMEM(pair_surfaces.shape, f32),
             pltpu.VMEM(WEIGHTS.shape, bf16),
-            pltpu.VMEM((G, AREA, number), f32),
+            pltpu.VMEM((2, 8, AREA, number), f32),
             pltpu.VMEM((KEEP, AREA, number), f32),
             pltpu.VMEM((2, table_rows, AREA), bf16),
             pltpu.VMEM((devices, cap, table_rows), bf16),
@@ -466,7 +500,7 @@
             pltpu.VMEM((width, AREA), f32),
             pltpu.VMEM((devices, 1, width), f32),
             pltpu.VMEM((everyone, 1, width), f32),
-            pltpu.SemaphoreType.DMA((2 + CHUNKS,)),
+            pltpu.SemaphoreType.DMA((SMALLS + 2 + CHUNKS,)),
             pltpu.SemaphoreType.DMA((devices,)),
             pltpu.SemaphoreType.DMA((devices,)),
             pltpu.SemaphoreType.DMA((devices,)),
@@ -475,12 +509,25 @@
             pltpu.SemaphoreType.DMA((everyone,)),
         ],
         compiler_params=pltpu.CompilerParams(
-            collective_id=0, has_side_effects=True, vmem_limit_bytes=60 * 1024 * 1024
+            collective_id=0, has_side_effects=True, vmem_limit_bytes=32 * 1024 * 1024
         ),
     )(
-        energies, triples, pair_surfaces, pair_slot, single_surfaces, modals, mode_slot.reshape(1, -1),
-        jnp.asarray(WEIGHTS), jnp.asarray(SMALL),
+        *[
+            pltpu.with_memory_space_constraint(x, pltpu.HBM)
+            for x in (
+                energies, triples.T, pair_surfaces, pair_slot, single_surfaces, modals, mode_slot.reshape(1, -1),
+                jnp.asarray(WEIGHTS), jnp.asarray(SMALL),
+            )
+        ]
     )
+    coefficients, energy, mean = pl.pallas_call(
+        write_kernel,
+        in_specs=[vmem] * 3,
+        out_specs=[hbm] * 3,
+        out_shape=results,
+        scratch_shapes=[pltpu.SemaphoreType.DMA((3,))],
+        compiler_params=pltpu.CompilerParams(vmem_limit_bytes=1024 * 1024),
+    )(*in_vmem)
     return coefficients, energy.reshape(number), mean
 
 

time: 38.8 us -> 33.2 us (0.86)
  local copies, waits for them, and re-layouts: 6.16 us -> 0 us
  Pallas kernels: 31.7 us -> 32.4 us
    unnamed x4 -> x0, local copies, waits for them, and re-layouts: 6.16 us -> none
    pallas_call x0 -> x1, Pallas kernels: none -> 1 us  [body(): pl.pallas_call(write_kernel, in_specs=[vmem] * 3, out_specs=[hbm] * 3, ou...]
where the time goes in v2:
time: 33.2 us; the launch traced here: 33 us
  Pallas kernels  32.4 us (98%)
  between operations  0.64 us (2%)
    pallas_call x1, Pallas kernels, body(): pl.pallas_call(functools.partial(kernel, devices=devices, groups=groups),...  31.4 us
    pallas_call x1, Pallas kernels, body(): pl.pallas_call(write_kernel, in_specs=[vmem] * 3, out_specs=[hbm] * 3, ou...  1 us

profile of v2, /device:TPU:0, one launch (start us, length us, event | category | flops | bytes accessed | tf_op | source)
XLA Modules:
  0.0 33.0 jit_solution(4423244834193444300)
XLA Ops:
  0.6 31.4 %shard_map.112 = (bf16[128,4096]{1,0:T(8,128)(2,1)S(1)}, f32[1,128]{1,0:T(1,128)S(1)}, f32[15,256]{1,0:T(8,128)S(1)}) custom-call(bf16[128,32768]{1,0:T(8,128)(2,1)} %energies.1, s32[3,128]{1,0:T(4,128)} %bitcast.3, f32[900,1024]{1,0:T(8,128)} %surfaces.1, s32[114,114]{1,0:T(8,128)} %pair_slot_hbm.1, f32[15,32]{1,0:T(8,128)} %singles_hbm.1, ...), custom_call_target="tpu_custom_call" | custom-call | tf_op jit(solution)/shard_map/pallas_call | solution.py:478
  32.0 1.0 %shard_map.113 = (bf16[128,4096]{1,0:T(8,128)(2,1)}, f32[1,128]{1,0:T(1,128)}, f32[15,256]{1,0:T(8,128)}) custom-call(bf16[128,4096]{1,0:T(8,128)(2,1)S(1)} %get-tuple-element.9.coefficients, f32[1,128]{1,0:T(1,128)S(1)} %get-tuple-element.10.energy, f32[15,256]{1,0:T(8,128)S(1)} %get-tuple-element.11.mean), custom_call_target="tpu_custom_call" | custom-call | tf_op jit(solution)/shard_map/pallas_call | solution.py:523

commit v3 on v2

--- a/solution.py
+++ b/solution.py
@@ -15,7 +15,6 @@
 HALF = G // 2
 LANES = 128
 STEPS = 4
-EARLY = 1
 CHUNKS = 8
 SMALLS = 6
 MESH = pl.DeviceIdType.MESH
@@ -109,7 +108,7 @@
     coefficients, energy_out, mean_out,
     triples, pair_slot, singles, modals, mode_slot, small,
     values, surf, weights, planes, acc, table, hits, answers, arrived, pair_t, padded, message, received,
-    modes_in, exp_modals, deep, moved, moments,
+    modes_of, mode_table, modes_in, exp_modals, deep, moved, moments,
     load_sem, send_msg, recv_msg, send_ans, recv_ans, send_mom, recv_mom,
     *, devices, groups,
 ):
@@ -122,6 +121,8 @@
     cap = answers.shape[1]
     slots = devices * cap
     bands = -(-mode_rows // 8)
+    held_rows = 8 * bands
+    spots_all = devices * held_rows
     offset = 2 * KEEP * bands
     width = moved.shape[2]
     everyone = devices * groups
@@ -200,9 +201,22 @@
     rank = (jnp.concatenate(ranks, axis=1) + 0.5).astype(jnp.int32)
     place = owner * cap + rank
     at_rank = ones_at(iota((LANES, needs), 0) == rank)
-    coarse = jnp.where(held, (local >> 4).astype(f32), 0.0).astype(bf16)
-    fine = jnp.where(held, (local & 15).astype(f32), 0.0).astype(bf16)
-    requests = 16.0 * nt(coarse, at_rank) + nt(fine, at_rank)
+    modes_hot = jnp.concatenate(on_hot, axis=1)
+    slot_ids = (nn(padded[2, 0:8, :].astype(bf16), modes_hot)[0:1, :] + 0.5).astype(jnp.int32)
+    homes = iota((devices, needs), 0)
+    home_row = total(jnp.where(slot_ids >= (homes + 1) * mode_rows, 1, 0), 0)
+    spot = home_row * held_rows + slot_ids - home_row * mode_rows
+    spots = [spot[:, p * number : (p + 1) * number] for p in range(3)]
+    lower, upper, third = [], [], []
+    for p, (one, two, three) in enumerate(((0, 1, 2), (0, 2, 1), (1, 2, 0))):
+        lower.append(jnp.where(flips[p], spots[two], spots[one]))
+        upper.append(jnp.where(flips[p], spots[one], spots[two]))
+        third.append(spots[three])
+    told = [local >> 4, local & 15] + [jnp.concatenate(x, axis=1) for x in (lower, upper, third)]
+    told = [jnp.where(held, x.astype(f32), 0.0).astype(bf16) for x in told]
+    sorted_told = nt(jnp.concatenate(told, axis=0), at_rank)
+    parts = [sorted_told[f * devices : (f + 1) * devices, :] for f in range(5)]
+    requests = [16.0 * parts[0] + parts[1]] + parts[2:]
 
     modes_in[...] = jnp.zeros_like(modes_in)
     modes_in[0:mode_rows, 0 : G * S] = modals[...]
@@ -218,10 +232,10 @@
     base = padded[3, 0:8, :]
     for q in range(1, bands):
         base = base + pltpu.roll(padded[3, 8 * q : 8 * q + 8, :], 2 * KEEP * q, 1)
-    asked = pltpu.roll(requests, offset, 1)
-    top = iota((8, LANES), 0) == 0
+    asked = [pltpu.roll(x, offset, 1) for x in requests]
+    blank = jnp.zeros((8 - len(asked), LANES), f32)
     for p in range(devices):
-        message[p] = base + jnp.where(top, asked[p : p + 1, :], 0.0)
+        message[p] = base + jnp.concatenate([x[p : p + 1, :] for x in asked] + [blank], axis=0)
     received[me] = message[me]
 
     pl.semaphore_wait(barrier, everyone - 1)
@@ -279,6 +293,67 @@
             at += count
         done += size
 
+    each_peer(lambda peer: message_copy(me, peer).wait_recv())
+    wanted = [received[p, f : f + 1, :] for f in range(4) for p in range(devices)]
+    if 4 * devices < LANES:
+        wanted.append(jnp.zeros((LANES - 4 * devices, LANES), f32))
+    wanted = (jnp.concatenate(wanted, axis=0).T[offset : offset + cap, :] + 0.5).astype(jnp.int32)
+    in_table = iota((capacity, table_rows), 1)
+    if cap > capacity:
+        hits[...] = jnp.zeros_like(hits)
+        modes_of[...] = jnp.zeros_like(modes_of)
+    for p in range(devices):
+        hits[p, 0:capacity, :] = ones_at(wanted[0:capacity, p : p + 1] == in_table)
+    all_hits = hits[...].reshape(slots, table_rows)
+    found = nn(all_hits, table[0]) + nn(all_hits, table[1])
+    answers[...] = found.reshape(devices, cap, AREA)
+    arrived[me] = answers[me]
+    each_peer(lambda peer: answer_copy(peer, me).start())
+
+    sent = received[...].reshape(devices * 8, LANES)
+    for q in range(bands):
+        turned = pltpu.roll(sent, LANES - 2 * KEEP * q, 1) if q else sent
+        mode_table[:, 8 * q : 8 * q + 8, :] = turned.reshape(devices, 8, LANES)
+    mode_rows_all = mode_table[...].reshape(spots_all, LANES)[:, 0 : 2 * KEEP]
+    tables_high, tables_low = split(mode_rows_all)
+    spot_hot = ones_at(iota((spots_all, needs), 0) == spot)
+    taken = tn(tables_high, spot_hot) + tn(tables_low, spot_hot)
+    ground = [taken[0:KEEP, p * number : (p + 1) * number] for p in range(3)]
+    single = [taken[KEEP : 2 * KEEP, p * number : (p + 1) * number] for p in range(3)]
+
+    in_spots = iota((capacity, spots_all), 1)
+    for f in range(3):
+        for p in range(devices):
+            column = wanted[0:capacity, (f + 1) * devices + p : (f + 1) * devices + p + 1]
+            modes_of[f, p, 0:capacity, :] = ones_at(column == in_spots)
+    columns = iota((KEEP, AREA), 1)
+    index = iota((KEEP, AREA), 0)
+    by_first = ones_at((columns >> 4) == index)
+    by_second = ones_at((columns & (KEEP - 1)) == index)
+    by_zero = ones_at(index == 0)
+    hot = [modes_of[f].reshape(slots, spots_all) for f in range(3)]
+
+    def spread_modes(which, pattern):
+        wide_high, wide_low = split(nn(tables_high[:, 0:KEEP], pattern) + nn(tables_low[:, 0:KEEP], pattern))
+        return nn(hot[which], wide_high) + nn(hot[which], wide_low)
+
+    def fold_orders(values, pattern):
+        high, low = split(values)
+        return nt(high, pattern) + nt(low, pattern)
+
+    ground_lower = spread_modes(0, by_first)
+    ground_upper = spread_modes(1, by_second)
+    scaled = found * spread_modes(2, by_zero)
+    takes = [
+        fold_orders(scaled * ground_upper, by_first),
+        fold_orders(scaled * ground_lower, by_second),
+        fold_orders(found * ground_upper * ground_lower, by_zero),
+    ]
+    owed = jnp.zeros((spots_all, KEEP), f32)
+    for f in range(3):
+        high, low = split(takes[f])
+        owed = owed + tn(hot[f], high) + tn(hot[f], low)
+
     for load in loads[SMALLS + 2 :]:
         load.wait()
 
@@ -299,72 +374,17 @@
             for c, value in enumerate(fit_orders(step, sums, differences)):
                 acc[c, span, :] = value if step == 0 else acc[c, span, :] + value
 
-    for step in range(EARLY):
+    for step in range(STEPS):
         inner_fit(step)
         if step:
             outer_fit(step - 1)
-
-    each_peer(lambda peer: message_copy(me, peer).wait_recv())
-    wanted = jnp.concatenate([received[p, 0:1, :] for p in range(devices)], axis=0)
-    wanted = jnp.concatenate([wanted, jnp.zeros((LANES - devices, LANES), f32)], axis=0)
-    wanted = (wanted.T[offset : offset + cap if offset + cap <= LANES else LANES, :] + 0.5).astype(jnp.int32)
-    in_table = iota((capacity, table_rows), 1)
-    if cap > capacity:
-        hits[...] = jnp.zeros_like(hits)
-    for p in range(devices):
-        hits[p, 0:capacity, :] = ones_at(wanted[0:capacity, p : p + 1] == in_table)
-    all_hits = hits[...].reshape(slots, table_rows)
-    found = nn(all_hits, table[0]) + nn(all_hits, table[1])
-    answers[...] = found.reshape(devices, cap, AREA)
-    arrived[me] = answers[me]
-    each_peer(lambda peer: answer_copy(peer, me).start())
-
-    modes_hot = jnp.concatenate(on_hot, axis=1)
-    slot_ids = (nn(padded[2, 0:8, :].astype(bf16), modes_hot)[0:1, :] + 0.5).astype(jnp.int32)
-    homes = iota((devices, needs), 0)
-    home = (slot_ids >= homes * mode_rows) & (slot_ids < (homes + 1) * mode_rows)
-    home_row = total(jnp.where(home, homes, 0), 0)
-    at_home = slot_ids - home_row * mode_rows
-    spot = home_row * 8 + (at_home & 7)
-    spot_hot = ones_at(iota((devices * 8, needs), 0) == spot)
-    tables_high, tables_low = split(received[...].reshape(devices * 8, LANES))
-    looked = tn(tables_high, spot_hot) + tn(tables_low, spot_hot)
-    band = at_home >> 3
-    taken = jnp.where(band == 0, looked[0 : 2 * KEEP], 0.0)
-    for q in range(1, bands):
-        taken = jnp.where(band == q, looked[2 * KEEP * q : 2 * KEEP * (q + 1)], taken)
-    ground = [taken[0:KEEP, p * number : (p + 1) * number] for p in range(3)]
-    single = [taken[KEEP : 2 * KEEP, p * number : (p + 1) * number] for p in range(3)]
-
-    for step in range(EARLY, STEPS):
-        inner_fit(step)
-        outer_fit(step - 1)
     outer_fit(STEPS - 1)
-
-    each_peer(lambda peer: answer_copy(me, peer).wait_recv())
-    place_hot = ones_at(iota((slots, needs), 0) == place)
-    arrived_high, arrived_low = split(arrived[...].reshape(slots, AREA))
-    ordered = tn(arrived_high, place_hot) + tn(arrived_low, place_hot)
-    for p in range(3):
-        pair_t[p] = ordered[:, p * number : (p + 1) * number]
-
-    def pair_rows_of(p, c):
-        straight = pair_t[p, c * KEEP : (c + 1) * KEEP, :]
-        turned_rows = pair_t[p, pl.ds(c, KEEP, stride=KEEP), :]
-        return jnp.where(flips[p], turned_rows, straight)
 
     first_row = iota((KEEP, number), 0) == 0
     for c in range(KEEP):
-        along_d = pair_rows_of(0, c)
-        along_e = pair_rows_of(1, c) + jnp.where(first_row, single[0][c : c + 1, :], 0.0)
-        if c == 0:
-            along_d = along_d + single[1]
-            along_e = along_e + single[2]
-            for d in range(KEEP):
-                acc[0, d * KEEP : (d + 1) * KEEP, :] -= pair_rows_of(2, d)
-        acc[c, pl.ds(0, KEEP, stride=KEEP), :] -= along_d
-        acc[c, 0:KEEP, :] -= along_e
-
+        here = jnp.where(first_row, single[0][c : c + 1, :], 0.0)
+        acc[c, 0:KEEP, :] -= here + single[2] if c == 0 else here
+    acc[0, pl.ds(0, KEEP, stride=KEEP), :] -= single[1]
     low3, high3 = ground[2][0:8], ground[2][8:16]
     rows1 = [ground[0][c : c + 1, :] for c in range(KEEP)]
     partial1 = [jnp.zeros((8, number), f32) for _ in range(KEEP)]
@@ -386,14 +406,18 @@
     field1 = jnp.concatenate([total(x, 0) for x in partial1], axis=0)
     field2 = jnp.concatenate(field2, axis=0)
     field3 = jnp.concatenate(field3, axis=0)
-    energy_out[...] = total(field1 * ground[0], 0)
+    energy = total(field1 * ground[0], 0)
 
     fields = jnp.concatenate([field1, field2, field3], axis=1)
-    fields = jnp.concatenate([fields] * (width // KEEP), axis=0)
-    of_row = (iota((width, needs), 0) >> 4) == at_home
-    fields_high, fields_low = split(jnp.where(of_row, fields, 0.0))
-    home_hot = ones_at(home)
-    sums = nt(home_hot, fields_high) + nt(home_hot, fields_low)
+    fields_high, fields_low = split(fields)
+    by_spot = nt(spot_hot, fields_high) + nt(spot_hot, fields_low) - owed
+    by_spot_high, by_spot_low = split(by_spot)
+    repeat = ones_at((iota((KEEP, width), 1) & (KEEP - 1)) == iota((KEEP, width), 0))
+    wide = nn(by_spot_high, repeat) + nn(by_spot_low, repeat)
+    wide_row = iota((spots_all, width), 0) & (held_rows - 1)
+    wide_high, wide_low = split(jnp.where(wide_row == (iota((spots_all, width), 1) >> 4), wide, 0.0))
+    of_home = ones_at((iota((devices, spots_all), 1) // held_rows) == iota((devices, spots_all), 0))
+    sums = nn(of_home, wide_high) + nn(of_home, wide_low)
     for p in range(devices):
         moved[p] = sums[p : p + 1, :]
     moments[flat] = moved[me]
@@ -407,25 +431,46 @@
 
     each_other(lambda there, peer: moment_copy(there, peer, flat).start())
 
-    for c in range(KEEP):
-        coefficients[:, c * AREA : (c + 1) * AREA] = acc[c].T.astype(bf16)
-
     rows16 = modes_in.shape[0]
     for g in range(G):
         exp_modals[g * rows16 : (g + 1) * rows16, 0:S] = modes_in[:, g * S : (g + 1) * S]
     pieces = exp_modals[:, 0:S]
-    columns = iota((S, AREA), 1)
-    index = iota((S, AREA), 0)
-    by_a = jnp.where((columns >> 4) == index, 1.0, 0.0)
-    by_b = jnp.where((columns & (S - 1)) == index, 1.0, 0.0)
     piece_high, piece_low = split(pieces)
-    by_a, by_b = by_a.astype(bf16), by_b.astype(bf16)
-    products = (nn(piece_high, by_a) + nn(piece_low, by_a)) * (nn(piece_high, by_b) + nn(piece_low, by_b))
+    products = (nn(piece_high, by_first) + nn(piece_low, by_first)) * (nn(piece_high, by_second) + nn(piece_low, by_second))
     products_high, products_low = split(products)
     tall = jnp.concatenate([spread] * (width // KEEP), axis=0)
     own_row = (iota(tall.shape, 1) & (rows16 - 1)) == (iota(tall.shape, 0) >> 4)
     tall_high, tall_low = split(jnp.where(own_row, tall, 0.0))
     deep[...] = nn(tall_high, products_high) + nn(tall_high, products_low) + nn(tall_low, products_high)
+
+    each_peer(lambda peer: answer_copy(me, peer).wait_recv())
+    place_hot = ones_at(iota((slots, needs), 0) == place)
+    arrived_high, arrived_low = split(arrived[...].reshape(slots, AREA))
+    ordered = tn(arrived_high, place_hot) + tn(arrived_low, place_hot)
+    for p in range(3):
+        pair_t[p] = ordered[:, p * number : (p + 1) * number]
+
+    def pair_rows_of(p, c):
+        straight = pair_t[p, c * KEEP : (c + 1) * KEEP, :]
+        turned_rows = pair_t[p, pl.ds(c, KEEP, stride=KEEP), :]
+        return jnp.where(flips[p], turned_rows, straight)
+
+    for c in range(KEEP):
+        acc[c, pl.ds(0, KEEP, stride=KEEP), :] -= pair_rows_of(0, c)
+        acc[c, 0:KEEP, :] -= pair_rows_of(1, c)
+        acc[0, c * KEEP : (c + 1) * KEEP, :] -= pair_rows_of(2, c)
+
+    for p, (one, two, three) in enumerate(((0, 1, 2), (0, 2, 1), (1, 2, 0))):
+        ground_low = jnp.where(flips[p], ground[two], ground[one])
+        ground_high = jnp.where(flips[p], ground[one], ground[two])
+        share = jnp.zeros((KEEP, number), f32)
+        for c in range(KEEP):
+            share = share + pair_t[p, c * KEEP : (c + 1) * KEEP, :] * ground_low[c : c + 1, :]
+        energy = energy - ground[three][0:1, :] * total(share * ground_high, 0)
+    energy_out[...] = energy
+
+    for c in range(KEEP):
+        coefficients[:, c * AREA : (c + 1) * AREA] = acc[c].T.astype(bf16)
 
     each_other(lambda there, peer: moment_copy(group, me, there * devices + peer).wait_recv())
     summed = moments[0]
@@ -463,6 +508,8 @@
     table_rows = round_up(pair_rows, 256)
     width = round_up(mode_rows * KEEP, LANES)
     rows16 = 16
+    held_rows = round_up(mode_rows, 8)
+    spots_all = devices * held_rows
     everyone = devices * groups
     vmem = pl.BlockSpec(memory_space=pltpu.VMEM)
     hbm = pl.BlockSpec(memory_space=pltpu.HBM)
@@ -495,6 +542,8 @@
             pltpu.VMEM((4, LANES, LANES), f32),
             pltpu.VMEM((devices, 8, LANES), f32),
             pltpu.VMEM((devices, 8, LANES), f32),
+            pltpu.VMEM((3, devices, cap, spots_all), bf16),
+            pltpu.VMEM((devices, held_rows, LANES), f32),
             pltpu.VMEM((rows16, SMALL.shape[1]), f32),
             pltpu.VMEM((G * rows16, LANES), f32),
             pltpu.VMEM((width, AREA), f32),

time: 33.2 us -> 28.4 us (0.86)
  Pallas kernels: 32.4 us -> 27.6 us
    pallas_call x1, Pallas kernels: 31.4 us -> 26.6 us  [body(): pl.pallas_call(functools.partial(kernel, devices=devices, groups=groups),...]
where the time goes in v3:
time: 28.4 us; the launch traced here: 28.3 us
  Pallas kernels  27.6 us (97%)
  between operations  0.64 us (2%)
    pallas_call x1, Pallas kernels, body(): pl.pallas_call(functools.partial(kernel, devices=devices, groups=groups),...  26.6 us
    pallas_call x1, Pallas kernels, body(): pl.pallas_call(write_kernel, in_specs=[vmem] * 3, out_specs=[hbm] * 3, ou...  1 us

profile of v3, /device:TPU:0, one launch (start us, length us, event | category | flops | bytes accessed | tf_op | source)
XLA Modules:
  0.0 28.3 jit_solution(11753528278076401707)
XLA Ops:
  0.6 26.6 %shard_map.112 = (bf16[128,4096]{1,0:T(8,128)(2,1)S(1)}, f32[1,128]{1,0:T(1,128)S(1)}, f32[15,256]{1,0:T(8,128)S(1)}) custom-call(bf16[128,32768]{1,0:T(8,128)(2,1)} %energies.1, s32[3,128]{1,0:T(4,128)} %bitcast.3, f32[900,1024]{1,0:T(8,128)} %surfaces.1, s32[114,114]{1,0:T(8,128)} %pair_slot_hbm.1, f32[15,32]{1,0:T(8,128)} %singles_hbm.1, ...), custom_call_target="tpu_custom_call" | custom-call | tf_op jit(solution)/shard_map/pallas_call | solution.py:525
  27.3 1.0 %shard_map.113 = (bf16[128,4096]{1,0:T(8,128)(2,1)}, f32[1,128]{1,0:T(1,128)}, f32[15,256]{1,0:T(8,128)}) custom-call(bf16[128,4096]{1,0:T(8,128)(2,1)S(1)} %get-tuple-element.9.coefficients, f32[1,128]{1,0:T(1,128)S(1)} %get-tuple-element.10.energy, f32[15,256]{1,0:T(8,128)S(1)} %get-tuple-element.11.mean), custom_call_target="tpu_custom_call" | custom-call | tf_op jit(solution)/shard_map/pallas_call | solution.py:572

commit v4 on v3

--- a/solution.py
+++ b/solution.py
@@ -15,6 +15,7 @@
 HALF = G // 2
 LANES = 128
 STEPS = 4
+EARLY = 1
 CHUNKS = 8
 SMALLS = 6
 MESH = pl.DeviceIdType.MESH
@@ -139,7 +140,9 @@
     for i in range(CHUNKS):
         span = pl.ds(i * part, part)
         pairs.append((energies.at[:, span], values.at[:, span]))
-    loads = [pltpu.make_async_copy(source, target, load_sem.at[i]) for i, (source, target) in enumerate(pairs)]
+    loads = [
+        pltpu.make_async_copy(source, target, load_sem.at[min(i, SMALLS + 2)]) for i, (source, target) in enumerate(pairs)
+    ]
     for load in loads[:SMALLS]:
         load.start()
 
@@ -205,7 +208,9 @@
     slot_ids = (nn(padded[2, 0:8, :].astype(bf16), modes_hot)[0:1, :] + 0.5).astype(jnp.int32)
     homes = iota((devices, needs), 0)
     home_row = total(jnp.where(slot_ids >= (homes + 1) * mode_rows, 1, 0), 0)
-    spot = home_row * held_rows + slot_ids - home_row * mode_rows
+    at_home = slot_ids - home_row * mode_rows
+    home_hot = ones_at(homes == home_row)
+    spot = home_row * held_rows + at_home
     spots = [spot[:, p * number : (p + 1) * number] for p in range(3)]
     lower, upper, third = [], [], []
     for p, (one, two, three) in enumerate(((0, 1, 2), (0, 2, 1), (1, 2, 0))):
@@ -240,19 +245,26 @@
 
     pl.semaphore_wait(barrier, everyone - 1)
 
-    def message_copy(peer, slot):
+    def exchange(source, target, send_sem, recv_sem, there, peer):
         return pltpu.make_async_remote_copy(
-            src_ref=message.at[peer], dst_ref=received.at[slot],
-            send_sem=send_msg.at[peer], recv_sem=recv_msg.at[slot],
-            device_id=(group, peer), device_id_type=MESH,
+            src_ref=source, dst_ref=target, send_sem=send_sem, recv_sem=recv_sem,
+            device_id=(there, peer), device_id_type=MESH,
         )
 
-    def answer_copy(peer, slot):
-        return pltpu.make_async_remote_copy(
-            src_ref=answers.at[peer], dst_ref=arrived.at[slot],
-            send_sem=send_ans.at[peer], recv_sem=recv_ans.at[slot],
-            device_id=(group, peer), device_id_type=MESH,
-        )
+    def message_copy(peer, slot, count=None):
+        rows = (lambda i: i) if count is None else (lambda i: pl.ds(0, count))
+        return exchange(message.at[rows(peer)], received.at[rows(slot)], send_msg, recv_msg, group, peer)
+
+    def answer_copy(peer, slot, count=None):
+        rows = (lambda i: i) if count is None else (lambda i: pl.ds(0, count))
+        return exchange(answers.at[rows(peer)], arrived.at[rows(slot)], send_ans, recv_ans, group, peer)
+
+    neighbour = lax.rem(me + 1, devices)
+    all_messages = message_copy(neighbour, 0, devices - 1)
+    all_answers = answer_copy(neighbour, 0, devices - 1)
+    all_moments = exchange(
+        moments.at[pl.ds(0, everyone - 1)], moments.at[pl.ds(0, everyone - 1)], send_mom, recv_mom, group, neighbour
+    )
 
     each_peer(lambda peer: message_copy(peer, me).start())
 
@@ -293,7 +305,31 @@
             at += count
         done += size
 
-    each_peer(lambda peer: message_copy(me, peer).wait_recv())
+    pltpu.make_async_copy(energies, values, load_sem.at[SMALLS + 2]).wait()
+
+    def inner_fit(step):
+        for i, j in enumerate(members(step)):
+            front = values[:, j * G * G : (j + 1) * G * G]
+            back = values[:, (G - 1 - j) * G * G : (G - j) * G * G]
+            both = jnp.concatenate([front, back], axis=0)
+            plane = nt(weights[0:AREA, :], both) + nt(weights[AREA : 2 * AREA, :], both)
+            planes[step % 2, i] = plane[:, :number] + plane[:, number:]
+            planes[step % 2, 4 + i] = plane[:, :number] - plane[:, number:]
+
+    def outer_fit(step):
+        for block in range(AREA // 8):
+            span = slice(block * 8, block * 8 + 8)
+            sums = [planes[step % 2, i, span, :] for i in range(4)]
+            differences = [planes[step % 2, 4 + i, span, :] for i in range(4)]
+            for c, value in enumerate(fit_orders(step, sums, differences)):
+                acc[c, span, :] = value if step == 0 else acc[c, span, :] + value
+
+    for step in range(EARLY):
+        inner_fit(step)
+        if step:
+            outer_fit(step - 1)
+
+    all_messages.wait_recv()
     wanted = [received[p, f : f + 1, :] for f in range(4) for p in range(devices)]
     if 4 * devices < LANES:
         wanted.append(jnp.zeros((LANES - 4 * devices, LANES), f32))
@@ -325,56 +361,49 @@
     for f in range(3):
         for p in range(devices):
             column = wanted[0:capacity, (f + 1) * devices + p : (f + 1) * devices + p + 1]
-            modes_of[f, p, 0:capacity, :] = ones_at(column == in_spots)
+            hot_row = ones_at(column == in_spots)
+            modes_of[f, p, 0:capacity, 0:spots_all] = hot_row
+            modes_of[f, p, 0:capacity, spots_all : 2 * spots_all] = hot_row
     columns = iota((KEEP, AREA), 1)
     index = iota((KEEP, AREA), 0)
     by_first = ones_at((columns >> 4) == index)
     by_second = ones_at((columns & (KEEP - 1)) == index)
     by_zero = ones_at(index == 0)
-    hot = [modes_of[f].reshape(slots, spots_all) for f in range(3)]
-
-    def spread_modes(which, pattern):
-        wide_high, wide_low = split(nn(tables_high[:, 0:KEEP], pattern) + nn(tables_low[:, 0:KEEP], pattern))
-        return nn(hot[which], wide_high) + nn(hot[which], wide_low)
+    patterns = jnp.concatenate([by_first, by_second, by_zero], axis=1)
+    wide_high, wide_low = split(nn(tables_high[:, 0:KEEP], patterns) + nn(tables_low[:, 0:KEEP], patterns))
+    wide_tables = jnp.concatenate([wide_high, wide_low], axis=0)
+    ground_lower, ground_upper, ground_third = [
+        nn(modes_of[f].reshape(slots, 2 * spots_all), wide_tables[:, f * AREA : (f + 1) * AREA]) for f in range(3)
+    ]
 
     def fold_orders(values, pattern):
         high, low = split(values)
         return nt(high, pattern) + nt(low, pattern)
 
-    ground_lower = spread_modes(0, by_first)
-    ground_upper = spread_modes(1, by_second)
-    scaled = found * spread_modes(2, by_zero)
+    seen_upper = found * ground_upper
     takes = [
-        fold_orders(scaled * ground_upper, by_first),
-        fold_orders(scaled * ground_lower, by_second),
-        fold_orders(found * ground_upper * ground_lower, by_zero),
-    ]
-    owed = jnp.zeros((spots_all, KEEP), f32)
+        fold_orders(seen_upper * ground_third, by_first),
+        fold_orders(found * ground_lower * ground_third, by_second),
+        fold_orders(seen_upper * ground_lower, by_zero),
+    ]
+    takes_high, takes_low = split(jnp.concatenate(takes, axis=0))
+    asked_spots = []
     for f in range(3):
-        high, low = split(takes[f])
-        owed = owed + tn(hot[f], high) + tn(hot[f], low)
-
-    for load in loads[SMALLS + 2 :]:
-        load.wait()
-
-    def inner_fit(step):
-        for i, j in enumerate(members(step)):
-            front = values[:, j * G * G : (j + 1) * G * G]
-            back = values[:, (G - 1 - j) * G * G : (G - j) * G * G]
-            both = jnp.concatenate([front, back], axis=0)
-            plane = nt(weights[0:AREA, :], both) + nt(weights[AREA : 2 * AREA, :], both)
-            planes[step % 2, i] = plane[:, :number] + plane[:, number:]
-            planes[step % 2, 4 + i] = plane[:, :number] - plane[:, number:]
-
-    def outer_fit(step):
-        for block in range(AREA // 8):
-            span = slice(block * 8, block * 8 + 8)
-            sums = [planes[step % 2, i, span, :] for i in range(4)]
-            differences = [planes[step % 2, 4 + i, span, :] for i in range(4)]
-            for c, value in enumerate(fit_orders(step, sums, differences)):
-                acc[c, span, :] = value if step == 0 else acc[c, span, :] + value
-
-    for step in range(STEPS):
+        for p in range(devices):
+            asked_spots.append(received[p, f + 1 : f + 2, offset : offset + cap])
+    asked_spots = jnp.concatenate(asked_spots, axis=1)
+    spot_rows = (asked_spots + 0.5).astype(jnp.int32)
+    turned_hot = ones_at(iota((spots_all, 3 * slots), 0) == spot_rows)
+    owed = nn(turned_hot, takes_high) + nn(turned_hot, takes_low)
+    owed_high, owed_low = split(owed)
+    repeat = ones_at((iota((KEEP, width), 1) & (KEEP - 1)) == iota((KEEP, width), 0))
+    owed = nn(owed_high, repeat) + nn(owed_low, repeat)
+    wide_row = iota((spots_all, width), 0) & (held_rows - 1)
+    owed_high, owed_low = split(jnp.where(wide_row == (iota((spots_all, width), 1) >> 4), owed, 0.0))
+    of_home = ones_at((iota((devices, spots_all), 1) // held_rows) == iota((devices, spots_all), 0))
+    owed = nn(of_home, owed_high) + nn(of_home, owed_low)
+
+    for step in range(EARLY, STEPS):
         inner_fit(step)
         if step:
             outer_fit(step - 1)
@@ -409,27 +438,16 @@
     energy = total(field1 * ground[0], 0)
 
     fields = jnp.concatenate([field1, field2, field3], axis=1)
-    fields_high, fields_low = split(fields)
-    by_spot = nt(spot_hot, fields_high) + nt(spot_hot, fields_low) - owed
-    by_spot_high, by_spot_low = split(by_spot)
-    repeat = ones_at((iota((KEEP, width), 1) & (KEEP - 1)) == iota((KEEP, width), 0))
-    wide = nn(by_spot_high, repeat) + nn(by_spot_low, repeat)
-    wide_row = iota((spots_all, width), 0) & (held_rows - 1)
-    wide_high, wide_low = split(jnp.where(wide_row == (iota((spots_all, width), 1) >> 4), wide, 0.0))
-    of_home = ones_at((iota((devices, spots_all), 1) // held_rows) == iota((devices, spots_all), 0))
-    sums = nn(of_home, wide_high) + nn(of_home, wide_low)
+    fields = jnp.concatenate([fields] * (width // KEEP), axis=0)
+    fields_high, fields_low = split(jnp.where((iota((width, needs), 0) >> 4) == at_home, fields, 0.0))
+    sums = nt(home_hot, fields_high) + nt(home_hot, fields_low) - owed
     for p in range(devices):
         moved[p] = sums[p : p + 1, :]
     moments[flat] = moved[me]
 
-    def moment_copy(there, peer, slot):
-        return pltpu.make_async_remote_copy(
-            src_ref=moved.at[peer], dst_ref=moments.at[slot],
-            send_sem=send_mom.at[there * devices + peer], recv_sem=recv_mom.at[slot],
-            device_id=(there, peer), device_id_type=MESH,
-        )
-
-    each_other(lambda there, peer: moment_copy(there, peer, flat).start())
+    each_other(
+        lambda there, peer: exchange(moved.at[peer], moments.at[flat], send_mom, recv_mom, there, peer).start()
+    )
 
     rows16 = modes_in.shape[0]
     for g in range(G):
@@ -441,9 +459,13 @@
     tall = jnp.concatenate([spread] * (width // KEEP), axis=0)
     own_row = (iota(tall.shape, 1) & (rows16 - 1)) == (iota(tall.shape, 0) >> 4)
     tall_high, tall_low = split(jnp.where(own_row, tall, 0.0))
-    deep[...] = nn(tall_high, products_high) + nn(tall_high, products_low) + nn(tall_low, products_high)
-
-    each_peer(lambda peer: answer_copy(me, peer).wait_recv())
+    deep_high, deep_low = split(
+        nn(tall_high, products_high) + nn(tall_high, products_low) + nn(tall_low, products_high)
+    )
+    deep[0] = deep_high
+    deep[1] = deep_low
+
+    all_answers.wait_recv()
     place_hot = ones_at(iota((slots, needs), 0) == place)
     arrived_high, arrived_low = split(arrived[...].reshape(slots, AREA))
     ordered = tn(arrived_high, place_hot) + tn(arrived_low, place_hot)
@@ -472,17 +494,18 @@
     for c in range(KEEP):
         coefficients[:, c * AREA : (c + 1) * AREA] = acc[c].T.astype(bf16)
 
-    each_other(lambda there, peer: moment_copy(group, me, there * devices + peer).wait_recv())
+    all_moments.wait_recv()
     summed = moments[0]
     for k in range(1, everyone):
         summed = summed + moments[k]
     chosen_rows = (iota((rows16, width), 1) >> 4) == iota((rows16, width), 0)
-    mean = nn(jnp.where(chosen_rows, summed, 0.0), deep[...], highest)
+    mean_high, mean_low = split(jnp.where(chosen_rows, summed, 0.0))
+    mean = nn(mean_high, deep[0]) + nn(mean_high, deep[1]) + nn(mean_low, deep[0])
     mean_out[...] = mean[0:mode_rows, :]
 
-    each_peer(lambda peer: message_copy(peer, me).wait_send())
-    each_peer(lambda peer: answer_copy(peer, me).wait_send())
-    each_other(lambda there, peer: moment_copy(there, peer, flat).wait_send())
+    all_messages.wait_send()
+    all_answers.wait_send()
+    all_moments.wait_send()
 
 
 def write_kernel(coefficients, energy, mean, coefficients_out, energy_out, mean_out, sems):
@@ -542,20 +565,15 @@
             pltpu.VMEM((4, LANES, LANES), f32),
             pltpu.VMEM((devices, 8, LANES), f32),
             pltpu.VMEM((devices, 8, LANES), f32),
-            pltpu.VMEM((3, devices, cap, spots_all), bf16),
+            pltpu.VMEM((3, devices, cap, 2 * spots_all), bf16),
             pltpu.VMEM((devices, held_rows, LANES), f32),
             pltpu.VMEM((rows16, SMALL.shape[1]), f32),
             pltpu.VMEM((G * rows16, LANES), f32),
-            pltpu.VMEM((width, AREA), f32),
+            pltpu.VMEM((2, width, AREA), bf16),
             pltpu.VMEM((devices, 1, width), f32),
             pltpu.VMEM((everyone, 1, width), f32),
-            pltpu.SemaphoreType.DMA((SMALLS + 2 + CHUNKS,)),
-            pltpu.SemaphoreType.DMA((devices,)),
-            pltpu.SemaphoreType.DMA((devices,)),
-            pltpu.SemaphoreType.DMA((devices,)),
-            pltpu.SemaphoreType.DMA((devices,)),
-            pltpu.SemaphoreType.DMA((everyone,)),
-            pltpu.SemaphoreType.DMA((everyone,)),
+            pltpu.SemaphoreType.DMA((SMALLS + 3,)),
+            *[pltpu.SemaphoreType.DMA] * 6,
         ],
         compiler_params=pltpu.CompilerParams(
             collective_id=0, has_side_effects=True, vmem_limit_bytes=32 * 1024 * 1024

time: 28.4 us -> 26.4 us (0.930)
  Pallas kernels: 27.6 us -> 25.6 us
    pallas_call x1, Pallas kernels: 26.6 us -> 24.6 us  [body(): pl.pallas_call(functools.partial(kernel, devices=devices, groups=groups),...]
where the time goes in v4:
time: 26.4 us; the launch traced here: 26.2 us
  Pallas kernels  25.6 us (97%)
  between operations  0.64 us (2%)
    pallas_call x1, Pallas kernels, body(): pl.pallas_call(functools.partial(kernel, devices=devices, groups=groups),...  24.6 us
    pallas_call x1, Pallas kernels, body(): pl.pallas_call(write_kernel, in_specs=[vmem] * 3, out_specs=[hbm] * 3, ou...  1 us

profile of v4, /device:TPU:0, one launch (start us, length us, event | category | flops | bytes accessed | tf_op | source)
XLA Modules:
  0.0 26.2 jit_solution(18030630375673697425)
XLA Ops:
  0.6 24.6 %shard_map.112 = (bf16[128,4096]{1,0:T(8,128)(2,1)S(1)}, f32[1,128]{1,0:T(1,128)S(1)}, f32[15,256]{1,0:T(8,128)S(1)}) custom-call(bf16[128,32768]{1,0:T(8,128)(2,1)} %energies.1, s32[3,128]{1,0:T(4,128)} %bitcast.3, f32[900,1024]{1,0:T(8,128)} %surfaces.1, s32[114,114]{1,0:T(8,128)} %pair_slot_hbm.1, f32[15,32]{1,0:T(8,128)} %singles_hbm.1, ...), custom_call_target="tpu_custom_call" | custom-call | tf_op jit(solution)/shard_map/pallas_call | solution.py:548
  25.2 1.0 %shard_map.113 = (bf16[128,4096]{1,0:T(8,128)(2,1)}, f32[1,128]{1,0:T(1,128)}, f32[15,256]{1,0:T(8,128)}) custom-call(bf16[128,4096]{1,0:T(8,128)(2,1)S(1)} %get-tuple-element.9.coefficients, f32[1,128]{1,0:T(1,128)S(1)} %get-tuple-element.10.energy, f32[15,256]{1,0:T(8,128)S(1)} %get-tuple-element.11.mean), custom_call_target="tpu_custom_call" | custom-call | tf_op jit(solution)/shard_map/pallas_call | solution.py:590

commit v5 on v4

--- a/solution.py
+++ b/solution.py
@@ -18,6 +18,7 @@
 EARLY = 1
 CHUNKS = 8
 SMALLS = 6
+UNROLLED = 8
 MESH = pl.DeviceIdType.MESH
 f32 = jnp.float32
 bf16 = jnp.bfloat16
@@ -43,6 +44,7 @@
 
 INNER = np.einsum("dh,el->dehl", FIT, FIT).reshape(AREA, G * G)
 WEIGHTS = np.concatenate(split_np(INNER), axis=0)
+ACROSS = np.concatenate(split_np(INNER.T), axis=1)
 SMALL = np.concatenate([np.repeat(COS, S, axis=1), FIT, np.zeros((KEEP, LANES - G))], axis=1).astype(np.float32)
 
 
@@ -105,10 +107,10 @@
 
 
 def kernel(
-    energies, triples_hbm, surfaces, pair_slot_hbm, singles_hbm, modals_hbm, mode_slot_hbm, weights_hbm, small_hbm,
+    energies, triples_hbm, surfaces, pair_slot_hbm, singles_hbm, modals_hbm, mode_slot_hbm, across_hbm, weights_hbm, small_hbm,
     coefficients, energy_out, mean_out,
     triples, pair_slot, singles, modals, mode_slot, small,
-    values, surf, weights, planes, acc, table, hits, answers, arrived, pair_t, padded, message, received,
+    values, surf, across, weights, planes, acc, table, answers, arrived, pair_t, padded, message, received,
     modes_of, mode_table, modes_in, exp_modals, deep, moved, moments,
     load_sem, send_msg, recv_msg, send_ans, recv_ans, send_mom, recv_mom,
     *, devices, groups,
@@ -134,23 +136,29 @@
     pairs = [
         (triples_hbm, triples), (pair_slot_hbm, pair_slot), (singles_hbm, singles),
         (modals_hbm, modals), (mode_slot_hbm, mode_slot), (small_hbm, small),
-        (weights_hbm, weights), (surfaces, surf),
+        (across_hbm, across), (surfaces, surf), (weights_hbm, weights),
     ]
     part = energies.shape[1] // CHUNKS
     for i in range(CHUNKS):
         span = pl.ds(i * part, part)
         pairs.append((energies.at[:, span], values.at[:, span]))
     loads = [
-        pltpu.make_async_copy(source, target, load_sem.at[min(i, SMALLS + 2)]) for i, (source, target) in enumerate(pairs)
-    ]
-    for load in loads[:SMALLS]:
-        load.start()
-
+        pltpu.make_async_copy(source, target, load_sem.at[min(i, SMALLS + 3)]) for i, (source, target) in enumerate(pairs)
+    ]
     barrier = pltpu.get_barrier_semaphore()
 
+    def after(position, k, size):
+        moved_on = position + k
+        return jnp.where(moved_on >= size, moved_on - size, moved_on)
+
     def each_peer(action):
+        if devices <= UNROLLED:
+            for k in range(1, devices):
+                action(after(me, k, devices))
+            return
+
         def step(k, carry):
-            action(lax.rem(me + k, devices))
+            action(after(me, k, devices))
             return carry
 
         lax.fori_loop(1, devices, step, 0)
@@ -158,14 +166,14 @@
     def each_other(action):
         each_peer(lambda peer: action(group, peer))
         for k in range(1, groups):
-            there = lax.rem(group + k, groups)
+            there = after(group, k, groups)
             action(there, me)
             each_peer(lambda peer: action(there, peer))
 
     each_other(
         lambda there, peer: pl.semaphore_signal(barrier, inc=1, device_id=(there, peer), device_id_type=MESH)
     )
-    for load in loads[SMALLS:]:
+    for load in loads[: SMALLS + 2]:
         load.start()
     for load in loads[:SMALLS]:
         load.wait()
@@ -243,6 +251,8 @@
         message[p] = base + jnp.concatenate([x[p : p + 1, :] for x in asked] + [blank], axis=0)
     received[me] = message[me]
 
+    for load in loads[SMALLS + 2 :]:
+        load.start()
     pl.semaphore_wait(barrier, everyone - 1)
 
     def exchange(source, target, send_sem, recv_sem, there, peer):
@@ -270,8 +280,6 @@
 
     loads[SMALLS].wait()
     loads[SMALLS + 1].wait()
-    w_high = weights[0:AREA, :]
-    w_low = weights[AREA : 2 * AREA, :]
     table_rows = table.shape[1]
     done = 0
     while done < table_rows:
@@ -297,7 +305,8 @@
                 table[:, at : done + size, :] = jnp.zeros((2, done + size - at, AREA), bf16)
                 continue
             high, low = split(piece)
-            fitted = nt(high, w_high) + nt(high, w_low) + nt(low, w_high)
+            both_parts = nn(high, across[...])
+            fitted = both_parts[:, 0:AREA] + both_parts[:, AREA : 2 * AREA] + nn(low, across[:, 0:AREA])
             count = piece.shape[0]
             part_high, part_low = split(fitted)
             table[0, at : at + count, :] = part_high
@@ -305,7 +314,8 @@
             at += count
         done += size
 
-    pltpu.make_async_copy(energies, values, load_sem.at[SMALLS + 2]).wait()
+    loads[SMALLS + 2].wait()
+    pltpu.make_async_copy(energies, values, load_sem.at[SMALLS + 3]).wait()
 
     def inner_fit(step):
         for i, j in enumerate(members(step)):
@@ -334,15 +344,18 @@
     if 4 * devices < LANES:
         wanted.append(jnp.zeros((LANES - 4 * devices, LANES), f32))
     wanted = (jnp.concatenate(wanted, axis=0).T[offset : offset + cap, :] + 0.5).astype(jnp.int32)
-    in_table = iota((capacity, table_rows), 1)
+    in_table = iota((cap, table_rows), 1)
     if cap > capacity:
-        hits[...] = jnp.zeros_like(hits)
         modes_of[...] = jnp.zeros_like(modes_of)
-    for p in range(devices):
-        hits[p, 0:capacity, :] = ones_at(wanted[0:capacity, p : p + 1] == in_table)
-    all_hits = hits[...].reshape(slots, table_rows)
-    found = nn(all_hits, table[0]) + nn(all_hits, table[1])
-    answers[...] = found.reshape(devices, cap, AREA)
+    found = []
+    half = max(1, devices // 2)
+    for start in range(0, devices, half):
+        rows_hot = jnp.concatenate(
+            [ones_at(wanted[:, p : p + 1] == in_table) for p in range(start, start + half)], axis=0
+        )
+        found.append(nn(rows_hot, table[0]) + nn(rows_hot, table[1]))
+        answers[start : start + half] = found[-1].reshape(half, cap, AREA)
+    found = jnp.concatenate(found, axis=0)
     arrived[me] = answers[me]
     each_peer(lambda peer: answer_copy(peer, me).start())
 
@@ -372,13 +385,21 @@
     patterns = jnp.concatenate([by_first, by_second, by_zero], axis=1)
     wide_high, wide_low = split(nn(tables_high[:, 0:KEEP], patterns) + nn(tables_low[:, 0:KEEP], patterns))
     wide_tables = jnp.concatenate([wide_high, wide_low], axis=0)
-    ground_lower, ground_upper, ground_third = [
-        nn(modes_of[f].reshape(slots, 2 * spots_all), wide_tables[:, f * AREA : (f + 1) * AREA]) for f in range(3)
-    ]
-
     def fold_orders(values, pattern):
         high, low = split(values)
         return nt(high, pattern) + nt(low, pattern)
+
+    def fit_step(step):
+        if step < STEPS:
+            inner_fit(step)
+        if step:
+            outer_fit(step - 1)
+
+    ground_lower, ground_upper, ground_third = [
+        nn(modes_of[f].reshape(slots, 2 * spots_all), wide_tables[:, f * AREA : (f + 1) * AREA]) for f in range(3)
+    ]
+
+    fit_step(EARLY)
 
     seen_upper = found * ground_upper
     takes = [
@@ -386,6 +407,8 @@
         fold_orders(found * ground_lower * ground_third, by_second),
         fold_orders(seen_upper * ground_lower, by_zero),
     ]
+    fit_step(EARLY + 1)
+
     takes_high, takes_low = split(jnp.concatenate(takes, axis=0))
     asked_spots = []
     for f in range(3):
@@ -402,12 +425,8 @@
     owed_high, owed_low = split(jnp.where(wide_row == (iota((spots_all, width), 1) >> 4), owed, 0.0))
     of_home = ones_at((iota((devices, spots_all), 1) // held_rows) == iota((devices, spots_all), 0))
     owed = nn(of_home, owed_high) + nn(of_home, owed_low)
-
-    for step in range(EARLY, STEPS):
-        inner_fit(step)
-        if step:
-            outer_fit(step - 1)
-    outer_fit(STEPS - 1)
+    for step in range(EARLY + 2, STEPS + 1):
+        fit_step(step)
 
     first_row = iota((KEEP, number), 0) == 0
     for c in range(KEEP):
@@ -547,18 +566,18 @@
     ]
     in_vmem = pl.pallas_call(
         functools.partial(kernel, devices=devices, groups=groups),
-        in_specs=[hbm] * 9,
+        in_specs=[hbm] * 10,
         out_specs=[vmem, vmem, vmem],
         out_shape=results,
         scratch_shapes=[
             *[pltpu.VMEM(shape, kind) for shape, kind in small_shapes],
             pltpu.VMEM(energies.shape, bf16),
             pltpu.VMEM(pair_surfaces.shape, f32),
+            pltpu.VMEM(ACROSS.shape, bf16),
             pltpu.VMEM(WEIGHTS.shape, bf16),
             pltpu.VMEM((2, 8, AREA, number), f32),
             pltpu.VMEM((KEEP, AREA, number), f32),
             pltpu.VMEM((2, table_rows, AREA), bf16),
-            pltpu.VMEM((devices, cap, table_rows), bf16),
             pltpu.VMEM((devices, cap, AREA), f32),
             pltpu.VMEM((devices, cap, AREA), f32),
             pltpu.VMEM((3, AREA, number), f32),
@@ -572,7 +591,7 @@
             pltpu.VMEM((2, width, AREA), bf16),
             pltpu.VMEM((devices, 1, width), f32),
             pltpu.VMEM((everyone, 1, width), f32),
-            pltpu.SemaphoreType.DMA((SMALLS + 3,)),
+            pltpu.SemaphoreType.DMA((SMALLS + 4,)),
             *[pltpu.SemaphoreType.DMA] * 6,
         ],
         compiler_params=pltpu.CompilerParams(
@@ -583,7 +602,7 @@
             pltpu.with_memory_space_constraint(x, pltpu.HBM)
             for x in (
                 energies, triples.T, pair_surfaces, pair_slot, single_surfaces, modals, mode_slot.reshape(1, -1),
-                jnp.asarray(WEIGHTS), jnp.asarray(SMALL),
+                jnp.asarray(ACROSS), jnp.asarray(WEIGHTS), jnp.asarray(SMALL),
             )
         ]
     )

time: 26.4 us -> 25.6 us (0.970)
  Pallas kernels: 25.6 us -> 24.8 us
    pallas_call x1, Pallas kernels: 24.6 us -> 23.8 us  [body(): pl.pallas_call(functools.partial(kernel, devices=devices, groups=groups),...]
where the time goes in v5:
time: 25.6 us; the launch traced here: 25.4 us
  Pallas kernels  24.8 us (97%)
  between operations  0.64 us (2%)
    pallas_call x1, Pallas kernels, body(): pl.pallas_call(functools.partial(kernel, devices=devices, groups=groups),...  23.8 us
    pallas_call x1, Pallas kernels, body(): pl.pallas_call(write_kernel, in_specs=[vmem] * 3, out_specs=[hbm] * 3, ou...  1 us

profile of v5, /device:TPU:0, one launch (start us, length us, event | category | flops | bytes accessed | tf_op | source)
XLA Modules:
  0.0 25.4 jit_solution(18316926859202376342)
XLA Ops:
  0.6 23.8 %shard_map.121 = (bf16[128,4096]{1,0:T(8,128)(2,1)S(1)}, f32[1,128]{1,0:T(1,128)S(1)}, f32[15,256]{1,0:T(8,128)S(1)}) custom-call(bf16[128,32768]{1,0:T(8,128)(2,1)} %energies.1, s32[3,128]{1,0:T(4,128)} %bitcast.3, f32[900,1024]{1,0:T(8,128)} %surfaces.1, s32[114,114]{1,0:T(8,128)} %pair_slot_hbm.1, f32[15,32]{1,0:T(8,128)} %singles_hbm.1, ...), custom_call_target="tpu_custom_call" | custom-call | tf_op jit(solution)/shard_map/pallas_call | solution.py:567
  24.4 1.0 %shard_map.122 = (bf16[128,4096]{1,0:T(8,128)(2,1)}, f32[1,128]{1,0:T(1,128)}, f32[15,256]{1,0:T(8,128)}) custom-call(bf16[128,4096]{1,0:T(8,128)(2,1)S(1)} %get-tuple-element.9.coefficients, f32[1,128]{1,0:T(1,128)S(1)} %get-tuple-element.10.energy, f32[15,256]{1,0:T(8,128)S(1)} %get-tuple-element.11.mean), custom_call_target="tpu_custom_call" | custom-call | tf_op jit(solution)/shard_map/pallas_call | solution.py:609

commit v6 on v5

--- a/solution.py
+++ b/solution.py
@@ -42,9 +42,8 @@
     return high, (values - high.astype(np.float32)).astype(jnp.bfloat16)
 
 
-INNER = np.einsum("dh,el->dehl", FIT, FIT).reshape(AREA, G * G)
-WEIGHTS = np.concatenate(split_np(INNER), axis=0)
-ACROSS = np.concatenate(split_np(INNER.T), axis=1)
+INNER = np.einsum("dh,el->hlde", FIT, FIT).reshape(G * G, AREA)
+ACROSS = np.concatenate(split_np(INNER), axis=1)
 SMALL = np.concatenate([np.repeat(COS, S, axis=1), FIT, np.zeros((KEEP, LANES - G))], axis=1).astype(np.float32)
 
 
@@ -107,10 +106,10 @@
 
 
 def kernel(
-    energies, triples_hbm, surfaces, pair_slot_hbm, singles_hbm, modals_hbm, mode_slot_hbm, across_hbm, weights_hbm, small_hbm,
+    energies, triples_hbm, surfaces, pair_slot_hbm, singles_hbm, modals_hbm, mode_slot_hbm, across_hbm, small_hbm,
     coefficients, energy_out, mean_out,
     triples, pair_slot, singles, modals, mode_slot, small,
-    values, surf, across, weights, planes, acc, table, answers, arrived, pair_t, padded, message, received,
+    values, surf, across, planes, acc, table, answers, arrived, pair_t, padded, message, received,
     modes_of, mode_table, modes_in, exp_modals, deep, moved, moments,
     load_sem, send_msg, recv_msg, send_ans, recv_ans, send_mom, recv_mom,
     *, devices, groups,
@@ -136,15 +135,17 @@
     pairs = [
         (triples_hbm, triples), (pair_slot_hbm, pair_slot), (singles_hbm, singles),
         (modals_hbm, modals), (mode_slot_hbm, mode_slot), (small_hbm, small),
-        (across_hbm, across), (surfaces, surf), (weights_hbm, weights),
+        (across_hbm, across), (surfaces, surf),
     ]
     part = energies.shape[1] // CHUNKS
     for i in range(CHUNKS):
         span = pl.ds(i * part, part)
         pairs.append((energies.at[:, span], values.at[:, span]))
     loads = [
-        pltpu.make_async_copy(source, target, load_sem.at[min(i, SMALLS + 3)]) for i, (source, target) in enumerate(pairs)
-    ]
+        pltpu.make_async_copy(source, target, load_sem.at[min(i, SMALLS + 2)]) for i, (source, target) in enumerate(pairs)
+    ]
+    for load in loads[: SMALLS + 2]:
+        load.start()
     barrier = pltpu.get_barrier_semaphore()
 
     def after(position, k, size):
@@ -173,7 +174,7 @@
     each_other(
         lambda there, peer: pl.semaphore_signal(barrier, inc=1, device_id=(there, peer), device_id_type=MESH)
     )
-    for load in loads[: SMALLS + 2]:
+    for load in loads[SMALLS + 2 :]:
         load.start()
     for load in loads[:SMALLS]:
         load.wait()
@@ -251,8 +252,6 @@
         message[p] = base + jnp.concatenate([x[p : p + 1, :] for x in asked] + [blank], axis=0)
     received[me] = message[me]
 
-    for load in loads[SMALLS + 2 :]:
-        load.start()
     pl.semaphore_wait(barrier, everyone - 1)
 
     def exchange(source, target, send_sem, recv_sem, there, peer):
@@ -314,17 +313,20 @@
             at += count
         done += size
 
-    loads[SMALLS + 2].wait()
-    pltpu.make_async_copy(energies, values, load_sem.at[SMALLS + 3]).wait()
+    pltpu.make_async_copy(energies, values, load_sem.at[SMALLS + 2]).wait()
 
     def inner_fit(step):
-        for i, j in enumerate(members(step)):
-            front = values[:, j * G * G : (j + 1) * G * G]
-            back = values[:, (G - 1 - j) * G * G : (G - j) * G * G]
-            both = jnp.concatenate([front, back], axis=0)
-            plane = nt(weights[0:AREA, :], both) + nt(weights[AREA : 2 * AREA, :], both)
-            planes[step % 2, i] = plane[:, :number] + plane[:, number:]
-            planes[step % 2, 4 + i] = plane[:, :number] - plane[:, number:]
+        js = members(step)
+        for first in range(0, 4, 1):
+            points = [g for j in js[first : first + 1] for g in (j, G - 1 - j)]
+            rows = jnp.concatenate([values[:, g * G * G : (g + 1) * G * G] for g in points], axis=0)
+            both = nn(rows, across[...])
+            plane = both[:, 0:AREA] + both[:, AREA : 2 * AREA]
+            for i in range(1):
+                front = plane[2 * i * number : (2 * i + 1) * number]
+                back = plane[(2 * i + 1) * number : (2 * i + 2) * number]
+                planes[step % 2, first + i] = (front + back).T
+                planes[step % 2, 4 + first + i] = (front - back).T
 
     def outer_fit(step):
         for block in range(AREA // 8):
@@ -357,7 +359,8 @@
         answers[start : start + half] = found[-1].reshape(half, cap, AREA)
     found = jnp.concatenate(found, axis=0)
     arrived[me] = answers[me]
-    each_peer(lambda peer: answer_copy(peer, me).start())
+    for k in sorted(range(1, devices), key=lambda k: abs(2 * k - devices)):
+        answer_copy(after(me, k, devices), me).start()
 
     sent = received[...].reshape(devices * 8, LANES)
     for q in range(bands):
@@ -566,7 +569,7 @@
     ]
     in_vmem = pl.pallas_call(
         functools.partial(kernel, devices=devices, groups=groups),
-        in_specs=[hbm] * 10,
+        in_specs=[hbm] * 9,
         out_specs=[vmem, vmem, vmem],
         out_shape=results,
         scratch_shapes=[
@@ -574,7 +577,6 @@
             pltpu.VMEM(energies.shape, bf16),
             pltpu.VMEM(pair_surfaces.shape, f32),
             pltpu.VMEM(ACROSS.shape, bf16),
-            pltpu.VMEM(WEIGHTS.shape, bf16),
             pltpu.VMEM((2, 8, AREA, number), f32),
             pltpu.VMEM((KEEP, AREA, number), f32),
             pltpu.VMEM((2, table_rows, AREA), bf16),
@@ -591,7 +593,7 @@
             pltpu.VMEM((2, width, AREA), bf16),
             pltpu.VMEM((devices, 1, width), f32),
             pltpu.VMEM((everyone, 1, width), f32),
-            pltpu.SemaphoreType.DMA((SMALLS + 4,)),
+            pltpu.SemaphoreType.DMA((SMALLS + 3,)),
             *[pltpu.SemaphoreType.DMA] * 6,
         ],
         compiler_params=pltpu.CompilerParams(
@@ -602,7 +604,7 @@
             pltpu.with_memory_space_constraint(x, pltpu.HBM)
             for x in (
                 energies, triples.T, pair_surfaces, pair_slot, single_surfaces, modals, mode_slot.reshape(1, -1),
-                jnp.asarray(ACROSS), jnp.asarray(WEIGHTS), jnp.asarray(SMALL),
+                jnp.asarray(ACROSS), jnp.asarray(SMALL),
             )
         ]
     )

time: 25.6 us -> 25 us (0.977)
  Pallas kernels: 24.8 us -> 24.2 us
    pallas_call x1, Pallas kernels: 23.8 us -> 23.2 us  [body(): pl.pallas_call(functools.partial(kernel, devices=devices, groups=groups),...]
where the time goes in v6:
time: 25 us; the launch traced here: 24.8 us
  Pallas kernels  24.2 us (97%)
  between operations  0.64 us (3%)
    pallas_call x1, Pallas kernels, body(): pl.pallas_call(functools.partial(kernel, devices=devices, groups=groups),...  23.2 us
    pallas_call x1, Pallas kernels, body(): pl.pallas_call(write_kernel, in_specs=[vmem] * 3, out_specs=[hbm] * 3, ou...  1 us

profile of v6, /device:TPU:0, one launch (start us, length us, event | category | flops | bytes accessed | tf_op | source)
XLA Modules:
  0.0 24.8 jit_solution(18197018916329596430)
XLA Ops:
  0.6 23.2 %shard_map.112 = (bf16[128,4096]{1,0:T(8,128)(2,1)S(1)}, f32[1,128]{1,0:T(1,128)S(1)}, f32[15,256]{1,0:T(8,128)S(1)}) custom-call(bf16[128,32768]{1,0:T(8,128)(2,1)} %energies.1, s32[3,128]{1,0:T(4,128)} %bitcast.3, f32[900,1024]{1,0:T(8,128)} %surfaces.1, s32[114,114]{1,0:T(8,128)} %pair_slot_hbm.1, f32[15,32]{1,0:T(8,128)} %singles_hbm.1, ...), custom_call_target="tpu_custom_call" | custom-call | tf_op jit(solution)/shard_map/pallas_call | solution.py:570
  23.8 1.0 %shard_map.113 = (bf16[128,4096]{1,0:T(8,128)(2,1)}, f32[1,128]{1,0:T(1,128)}, f32[15,256]{1,0:T(8,128)}) custom-call(bf16[128,4096]{1,0:T(8,128)(2,1)S(1)} %get-tuple-element.9.coefficients, f32[1,128]{1,0:T(1,128)S(1)} %get-tuple-element.10.energy, f32[15,256]{1,0:T(8,128)S(1)} %get-tuple-element.11.mean), custom_call_target="tpu_custom_call" | custom-call | tf_op jit(solution)/shard_map/pallas_call | solution.py:611

commit v7 on v6

--- a/solution.py
+++ b/solution.py
@@ -516,17 +516,18 @@
     for c in range(KEEP):
         coefficients[:, c * AREA : (c + 1) * AREA] = acc[c].T.astype(bf16)
 
+    all_messages.wait_send()
+    all_answers.wait_send()
     all_moments.wait_recv()
-    summed = moments[0]
-    for k in range(1, everyone):
-        summed = summed + moments[k]
+    terms = [moments[k] for k in range(everyone)]
+    while len(terms) > 1:
+        terms = [sum(terms[i + 1 : i + 2], terms[i]) for i in range(0, len(terms), 2)]
+    summed = terms[0]
     chosen_rows = (iota((rows16, width), 1) >> 4) == iota((rows16, width), 0)
     mean_high, mean_low = split(jnp.where(chosen_rows, summed, 0.0))
     mean = nn(mean_high, deep[0]) + nn(mean_high, deep[1]) + nn(mean_low, deep[0])
     mean_out[...] = mean[0:mode_rows, :]
 
-    all_messages.wait_send()
-    all_answers.wait_send()
     all_moments.wait_send()
 
 

time: 25 us -> 25 us (level)
  no operation moved by 1% of the time
where the time goes in v7:
time: 25 us; the launch traced here: 24.8 us
  Pallas kernels  24.2 us (97%)
  between operations  0.64 us (3%)
    pallas_call x1, Pallas kernels, body(): pl.pallas_call(functools.partial(kernel, devices=devices, groups=groups),...  23.2 us
    pallas_call x1, Pallas kernels, body(): pl.pallas_call(write_kernel, in_specs=[vmem] * 3, out_specs=[hbm] * 3, ou...  1 us

profile of v7, /device:TPU:0, one launch (start us, length us, event | category | flops | bytes accessed | tf_op | source)
XLA Modules:
  0.0 24.8 jit_solution(9235804557157806310)
XLA Ops:
  0.6 23.2 %shard_map.112 = (bf16[128,4096]{1,0:T(8,128)(2,1)S(1)}, f32[1,128]{1,0:T(1,128)S(1)}, f32[15,256]{1,0:T(8,128)S(1)}) custom-call(bf16[128,32768]{1,0:T(8,128)(2,1)} %energies.1, s32[3,128]{1,0:T(4,128)} %bitcast.3, f32[900,1024]{1,0:T(8,128)} %surfaces.1, s32[114,114]{1,0:T(8,128)} %pair_slot_hbm.1, f32[15,32]{1,0:T(8,128)} %singles_hbm.1, ...), custom_call_target="tpu_custom_call" | custom-call | tf_op jit(solution)/shard_map/pallas_call | solution.py:571
  23.8 1.0 %shard_map.113 = (bf16[128,4096]{1,0:T(8,128)(2,1)}, f32[1,128]{1,0:T(1,128)}, f32[15,256]{1,0:T(8,128)}) custom-call(bf16[128,4096]{1,0:T(8,128)(2,1)S(1)} %get-tuple-element.9.coefficients, f32[1,128]{1,0:T(1,128)S(1)} %get-tuple-element.10.energy, f32[15,256]{1,0:T(8,128)S(1)} %get-tuple-element.11.mean), custom_call_target="tpu_custom_call" | custom-call | tf_op jit(solution)/shard_map/pallas_call | solution.py:612
